TPU v7x, 32 devices: a whole 2x2x4 slice. The times are simulated.
32 devices in a mesh: ctx: 4 (over x, core), fsdp: 8 (over z, y).
Axes of the slice: x: 2, y: 2, z: 4, core: 2. Of those that a mesh axis runs over, the one named last changes fastest.
Arguments:
- hidden_in: bfloat16 [8, 512, 1536], P('fsdp', 'ctx'), may hold values from -6 to 6
- segments: int32 [8, 512], P('fsdp', 'ctx'), may hold values from 0 to 3, never falling along the last dimension, each value on 1 to 384 neighbouring positions
- w_query: bfloat16 [1536, 1536], P('fsdp'), may hold values from -0.15625 to 0.15625
- w_key: bfloat16 [1536, 768], P('fsdp'), may hold values from -0.15625 to 0.15625
- w_value: bfloat16 [1536, 768], P('fsdp'), may hold values from -0.15625 to 0.15625
- w_out: bfloat16 [1536, 1536], P('fsdp'), may hold values from -0.875 to 0.875
- w_gate: bfloat16 [1536, 4096], P('fsdp'), may hold values from -0.15625 to 0.15625
- w_up: bfloat16 [1536, 4096], P('fsdp'), may hold values from -0.15625 to 0.15625
- w_down: bfloat16 [4096, 1536], P('fsdp'), may hold values from -0.09375 to 0.09375
- attn_gain: bfloat16 [1536], P('fsdp'), may hold values from 0.5 to 1.5
- ffn_gain: bfloat16 [1536], P('fsdp'), may hold values from 0.5 to 1.5
- grad_out: bfloat16 [8, 512, 1536], P('fsdp', 'ctx'), may hold values from -6 to 6
Outputs:
- output: bfloat16 [8, 512, 1536], P('fsdp', 'ctx')
- grad_in: float32 [8, 512, 1536], P('fsdp', 'ctx')
- grad_w_query: float32 [1536, 1536], P(('ctx', 'fsdp'))
- grad_w_key: float32 [1536, 768], P(('ctx', 'fsdp'))
- grad_w_value: float32 [1536, 768], P(('ctx', 'fsdp'))
- grad_w_out: float32 [1536, 1536], P(('ctx', 'fsdp'))
- grad_w_gate: float32 [1536, 4096], P(('ctx', 'fsdp'))
- grad_w_up: float32 [1536, 4096], P(('ctx', 'fsdp'))
- grad_w_down: float32 [4096, 1536], P(('ctx', 'fsdp'))
- grad_attn_gain: float32 [1536], P(('ctx', 'fsdp'))
- grad_ffn_gain: float32 [1536], P(('ctx', 'fsdp'))
Inputs may be any that keep to these rules, and one draw needn't show every extreme that they name: `segments`: segment numbers never fall along a sequence.
All inputs are finite; a program needn't handle non-finite values.
Results may differ from a plain program's by a relative error of at most 0.014.
Values may be sent and summed in bfloat16 or wider, within the bound.
A program may use at most 192 MiB of HBM per device.

v0:
```python
import functools
import math

import jax
import jax.numpy as jnp
from jax import lax
from jax.experimental import pallas as pl
from jax.experimental.pallas import tpu as pltpu
from jax.sharding import PartitionSpec as P

HEADS = 16
KV_HEADS = 8
HEAD_DIM = 96
EPS = 1e-05
ROPE_BASE = 100000.0

AHEAD = 4
MESH = pl.DeviceIdType.MESH
ANY = pl.BlockSpec(memory_space=pl.ANY)
VMEM = pl.BlockSpec(memory_space=pltpu.VMEM)
DMA = pltpu.SemaphoreType.DMA
LOW = jnp.bfloat16
WIDE = jnp.float32


def remote(src, dst, send, recv, **where):
    return pltpu.make_async_remote_copy(
        src_ref=src,
        dst_ref=dst,
        send_sem=send,
        recv_sem=recv,
        device_id=where,
        device_id_type=MESH,
    )


def place(fsdp_size):
    f, c = lax.axis_index("fsdp"), lax.axis_index("ctx")
    return f, c, f // 2, f % 2, fsdp_size // 2


def greet(fsdp_size):
    f, c, z, y, depth = place(fsdp_size)
    barrier = pltpu.get_barrier_semaphore()
    for bits in (1, 2, 3):
        pl.semaphore_signal(barrier, inc=1, device_id={"ctx": c ^ bits}, device_id_type=MESH)
    pl.semaphore_signal(barrier, inc=1, device_id={"fsdp": f ^ 1}, device_id_type=MESH)
    for step in (1, -1):
        near = z + step

        @pl.when((near >= 0) & (near < depth))
        def _():
            pl.semaphore_signal(
                barrier, inc=1, device_id={"fsdp": near * 2 + y}, device_id_type=MESH
            )

    pl.semaphore_wait(barrier, 4 + jnp.minimum(z, 1) + jnp.minimum(depth - 1 - z, 1))


class LineGather:
    def __init__(self, ctx_size, fsdp_size, masked, blocks, owns, fulls, stages, sems):
        self.sizes = ctx_size, fsdp_size
        self.f, self.c, self.z, self.y, self.depth = place(fsdp_size)
        self.masked, self.blocks = masked, blocks
        self.owns, self.fulls, self.stages = owns, fulls, stages
        self.z_send, self.z_recv, self.y_send, self.y_recv, self.local = sems
        self.beside_done = set()

    @staticmethod
    def scratch(fsdp_size, arrays, count):
        depth = fsdp_size // 2
        return [
            *[pltpu.VMEM(a.shape, a.dtype) for a in arrays],
            DMA((count, 2, depth - 1)),
            DMA((count, 2, depth - 1)),
            DMA((count, 2 * depth - 1)),
            DMA((count, 2 * depth - 1)),
            DMA((len(arrays),)),
        ]

    def held(self, a, row):
        there = (row >= 0) & (row < self.depth)
        if self.masked[a]:
            span = self.depth // self.sizes[0]
            there = there & (row >= self.c * span) & (row < (self.c + 1) * span)
        return there

    def entry(self, a, row, column):
        base = self.c * (self.sizes[1] // self.sizes[0]) if self.masked[a] else 0
        return row * 2 + column - base

    def spot(self, b, row, column):
        a, low, size = self.blocks[b]
        return self.fulls[a].at[self.entry(a, row, column), pl.ds(low, size)]

    def source(self, b, row):
        a, low, size = self.blocks[b]
        return self.owns[a].at[pl.ds(low, size)] if row is None else self.spot(b, row, self.y)

    def z_copy(self, b, way, hop):
        step = 1 if way == 0 else -1
        row = self.z - step * (hop - 1)
        near = self.z + step
        copy = remote(
            self.source(b, None if hop == 1 else row),
            self.spot(b, row, self.y),
            self.z_send.at[b, way, hop - 1],
            self.z_recv.at[b, way, hop - 1],
            fsdp=near * 2 + self.y,
        )
        return copy, self.held(self.blocks[b][0], row) & (near >= 0) & (near < self.depth)

    def row_of(self, slot):
        return self.z - slot if slot < self.depth else self.z + (slot - self.depth + 1)

    def y_copy(self, b, slot):
        row = self.row_of(slot)
        copy = remote(
            self.source(b, row if slot else None),
            self.spot(b, row, self.y),
            self.y_send.at[b, slot],
            self.y_recv.at[b, slot],
            fsdp=self.f ^ 1,
        )
        return copy, self.held(self.blocks[b][0], row)

    @staticmethod
    def begin(pair):
        pl.when(pair[1])(lambda: pair[0].start())

    def send_own(self, b):
        self.begin(self.z_copy(b, 0, 1))
        self.begin(self.z_copy(b, 1, 1))
        self.begin(self.y_copy(b, 0))

    def local_in(self, a):
        return pltpu.make_async_copy(self.owns[a], self.stages[a], self.local.at[a])

    def local_out(self, a):
        spot = self.fulls[a].at[self.entry(a, self.z, self.y)]
        return pltpu.make_async_copy(self.stages[a], spot, self.local.at[a])

    def start(self):
        for a in range(len(self.owns)):
            self.local_in(a).start()
        for b in range(min(2, len(self.blocks))):
            self.send_own(b)
        for a in range(len(self.owns)):
            self.local_in(a).wait()
            pl.when(self.held(a, self.z))(lambda a=a: self.local_out(a).start())

    def step(self, b, hop):
        a = self.blocks[b][0]
        for way in (0, 1):
            row = self.z - hop if way == 0 else self.z + hop

            @pl.when(self.held(a, row))
            def _():
                remote(
                    self.source(b, None),
                    self.spot(b, row, self.y),
                    self.z_send.at[b, way, hop - 1],
                    self.z_recv.at[b, way, hop - 1],
                    fsdp=self.f ^ 1,
                ).wait_recv()

            if hop + 1 < self.depth:
                self.begin(self.z_copy(b, way, hop + 1))
            self.begin(self.y_copy(b, hop if way == 0 else self.depth - 1 + hop))
        if hop == 1 and b + 2 < len(self.blocks):
            self.send_own(b + 2)

    def steps(self):
        return [
            functools.partial(self.step, b, hop)
            for b in range(len(self.blocks))
            for hop in range(1, self.depth)
        ]

    def wait_local(self, a):
        pl.when(self.held(a, self.z))(lambda: self.local_out(a).wait())

    def wait_beside(self, b):
        if b in self.beside_done:
            return
        self.beside_done.add(b)
        for slot in range(2 * self.depth - 1):
            row = self.row_of(slot)

            @pl.when(self.held(self.blocks[b][0], row))
            def _():
                remote(
                    self.source(b, None),
                    self.spot(b, row, 1 - self.y),
                    self.y_send.at[b, slot],
                    self.y_recv.at[b, slot],
                    fsdp=self.f ^ 1,
                ).wait_recv()

    def finish(self, local_done=()):
        for b in range(len(self.blocks)):
            self.wait_beside(b)
        pairs = []
        for b in range(len(self.blocks)):
            for hop in range(1, self.depth):
                pairs += [self.z_copy(b, 0, hop), self.z_copy(b, 1, hop)]
            pairs += [self.y_copy(b, slot) for slot in range(2 * self.depth - 1)]
        for copy, there in pairs:
            pl.when(there)(lambda copy=copy: copy.wait_send())
        for a in range(len(self.owns)):
            if a not in local_done:
                self.wait_local(a)


def weave(steps, inserts):
    for i, step in enumerate(steps):
        for extra in inserts.get(i, ()):
            extra()
        step()
    for i in sorted(inserts):
        if i >= len(steps):
            for extra in inserts[i]:
                extra()


def row_loop(total, body, rows=16):
    rows = rows if total % rows == 0 else total

    def run(step, carry):
        body(pl.ds(pl.multiple_of(step * rows, rows), rows))
        return carry

    lax.fori_loop(0, total // rows, run, 0)


def add_rows(out_ref, terms):
    shape = out_ref.shape
    leads = [None] if len(shape) == 2 else list(range(shape[0]))

    def body(at):
        for lead in leads:
            index = (at,) if lead is None else (lead, at)
            value = None
            for ref in terms:
                part = ref[index].astype(WIDE)
                value = part if value is None else value + part
            out_ref[index] = value.astype(out_ref.dtype)

    row_loop(shape[-2], body)


def first_kernel(ctx_size, fsdp_size, n_blocks, n_runs, *refs):
    owns, runs, refs = refs[:n_blocks], refs[n_blocks : n_blocks + n_runs], refs[n_blocks + n_runs :]
    fulls, alls, refs = refs[:n_blocks], refs[n_blocks : n_blocks + n_runs], refs[n_blocks + n_runs :]
    stages, sems, refs = refs[:n_blocks], refs[n_blocks : n_blocks + 5], refs[n_blocks + 5 :]
    stage_runs, (c_send, c_recv, local) = refs[:n_runs], refs[n_runs:]
    c = lax.axis_index("ctx")
    blocks = [(a, 0, owns[a].shape[0]) for a in range(n_blocks)]
    line = LineGather(
        ctx_size, fsdp_size, (False,) * n_blocks, blocks, owns, fulls, stages, sems
    )
    greet(fsdp_size)

    def run_copy(r, bits):
        slot = (0, 2, 1, 3)[bits]
        return remote(
            runs[r], alls[r].at[slot], c_send.at[r, bits - 1], c_recv.at[r, bits - 1], ctx=c ^ bits
        )

    line.start()
    for r in range(n_runs):
        pltpu.make_async_copy(runs[r], stage_runs[r], local.at[r]).start()
        for bits in (2, 1, 3):
            run_copy(r, bits).start()
    for r in range(n_runs):
        pltpu.make_async_copy(runs[r], stage_runs[r], local.at[r]).wait()
        pltpu.make_async_copy(stage_runs[r], alls[r].at[0], local.at[r]).start()
    weave(line.steps(), {})
    line.finish()
    for r in range(n_runs):
        for bits in (2, 1, 3):
            run_copy(r, bits).wait()
        pltpu.make_async_copy(stage_runs[r], alls[r].at[0], local.at[r]).wait()


def gather_first(ctx_size, fsdp_size, collective_id, blocks, runs):
    n_blocks, n_runs = len(blocks), len(runs)
    outs = [jax.ShapeDtypeStruct((fsdp_size, *b.shape), b.dtype) for b in blocks]
    outs += [jax.ShapeDtypeStruct((ctx_size, *r.shape), r.dtype) for r in runs]
    results = pl.pallas_call(
        functools.partial(first_kernel, ctx_size, fsdp_size, n_blocks, n_runs),
        out_shape=tuple(outs),
        in_specs=[ANY] * (n_blocks + n_runs),
        out_specs=(ANY,) * (n_blocks + n_runs),
        scratch_shapes=[
            *LineGather.scratch(fsdp_size, blocks, n_blocks),
            *[pltpu.VMEM(r.shape, r.dtype) for r in runs],
            DMA((n_runs, 3)),
            DMA((n_runs, 3)),
            DMA((n_runs,)),
        ],
        compiler_params=pltpu.CompilerParams(collective_id=collective_id, has_side_effects=True),
    )(*blocks, *runs)
    return results[:n_blocks], results[n_blocks:]


def second_kernel(ctx_size, fsdp_size, blocks, heads, kv_heads, *refs):
    owns, refs = refs[:3], refs[3:]
    query, key, value, bias, hidden, gain, refs = *refs[:6], refs[6:]
    fulls, refs = refs[:3], refs[3:]
    rows_out, log_out, mid_out, normed, refs = *refs[:4], refs[4:]
    stages, sems, refs = refs[:3], refs[3:8], refs[8:]
    w_pad, kept, core_out, core_in, pair, pair_in, c_send, c_recv, w_sem = refs
    c = lax.axis_index("ctx")
    line = LineGather(ctx_size, fsdp_size, (True, False, True), blocks, owns, fulls, stages, sems)
    tokens, half = query.shape[1], hidden.shape[0]
    run_len = half // 2
    scale = HEAD_DIM**-0.5
    tile = 128

    def attention(part):
        def body(i, carry):
            h = i // (tokens // tile)
            r = i % (tokens // tile)
            at = pl.ds(pl.multiple_of(r * tile, tile), tile)
            g = h // (heads // kv_heads)
            s = lax.dot_general(
                query[h, at], key[g], (((1,), (1,)), ((), ())), preferred_element_type=WIDE
            )
            s = s * scale + bias[at]
            top = jnp.max(s, axis=-1, keepdims=True)
            log = top + jnp.log(jnp.sum(jnp.exp(s - top), axis=-1, keepdims=True))
            p = jnp.exp(s - log).astype(LOW)
            mixed = jnp.dot(p, value[g], preferred_element_type=WIDE)
            rows_out[at, pl.ds(pl.multiple_of(h * 128, 128), 128)] = mixed.astype(LOW)
            log_out[h, at] = log
            return carry

        count = heads * (tokens // tile)
        lax.fori_loop(part * count // 2, (part + 1) * count // 2, body, 0)

    def exchange(index, src, dst, bits):
        return remote(src, dst, c_send.at[index], c_recv.at[index], ctx=c ^ bits)

    to_core = exchange(0, core_out, core_in, 1)
    to_x = exchange(1, pair, pair_in, 2)
    give = exchange(2, normed.at[pl.ds(0, half)], normed.at[pl.ds(half, half)], 1)

    shard = owns[0].shape[0]
    piece = min(shard, HEAD_DIM)
    moves = []
    for at in range(0, heads * HEAD_DIM, piece):
        to = at // HEAD_DIM * 128 + at % HEAD_DIM
        src = fulls[0].at[at // shard, pl.ds(at % shard, piece)]
        moves.append(pltpu.make_async_copy(src, w_pad.at[pl.ds(to, piece)], w_sem.at[len(moves)]))

    def load_out():
        line.wait_beside(0)
        line.wait_local(0)
        for move in moves:
            move.start()
        for h in range(heads):
            w_pad[pl.ds(h * 128 + HEAD_DIM, 128 - HEAD_DIM)] = jnp.zeros(
                (128 - HEAD_DIM, w_pad.shape[1]), LOW
            )
        for move in moves:
            move.wait()

    def project():
        def far(at):
            value_rows = rows_out[pl.ds(pl.multiple_of(at.start + half, tile), tile)]
            core_out[at] = jnp.dot(value_rows, w_pad[...], preferred_element_type=WIDE).astype(LOW)

        row_loop(half, far, tile)
        to_core.start()

        def near(at):
            kept[at] = jnp.dot(rows_out[at], w_pad[...], preferred_element_type=WIDE)

        row_loop(half, near, tile)

    def meet_core():
        to_core.wait_recv()
        add_rows(pair, (kept, core_in))
        to_x.start()

    def meet_x():
        to_x.wait_recv()
        for block in (0, 1):

            def body(at, block=block):
                here = pl.ds(pl.multiple_of(at.start + block * run_len, 16), 16)
                there = pl.ds(pl.multiple_of(at.start + (1 - block) * run_len, 16), 16)
                mid = hidden[here].astype(WIDE) + (
                    pair[here].astype(WIDE) + pair_in[there].astype(WIDE)
                )
                mid_out[here] = mid
                scaled = mid * inverse_rms(mid)
                normed[here] = (scaled * gain[0:1]).astype(LOW)

            row_loop(run_len, body)
        give.start()

    greet(fsdp_size)
    line.start()
    steps = line.steps()
    hops = fsdp_size // 2 - 1
    inserts = {
        0: [lambda: attention(0), lambda: attention(1)],
        hops + 2: [load_out, project],
        2 * hops: [meet_core],
        2 * hops + 2: [meet_x],
    }
    weave(steps, inserts)
    line.finish(local_done=(0,))
    give.wait_recv()
    for copy in (to_core, to_x, give):
        copy.wait_send()


def gather_second(ctx_size, fsdp_size, collective_id, shards, query, key, value, bias, hidden, gain):
    heads, tokens, _ = query.shape
    half, width = hidden.shape
    counts = (fsdp_size // ctx_size, fsdp_size, fsdp_size // ctx_size)
    pieces = (1, 2, 4)
    blocks = []
    for a, shard in enumerate(shards):
        size = shard.shape[0] // pieces[a]
        blocks += [(a, i * size, size) for i in range(pieces[a])]
    outs = [jax.ShapeDtypeStruct((n, *s.shape), s.dtype) for n, s in zip(counts, shards)]
    outs += [
        jax.ShapeDtypeStruct((tokens, heads * 128), LOW),
        jax.ShapeDtypeStruct((heads, tokens, 1), WIDE),
        jax.ShapeDtypeStruct((half, width), WIDE),
        jax.ShapeDtypeStruct((tokens, width), LOW),
    ]
    return pl.pallas_call(
        functools.partial(
            second_kernel, ctx_size, fsdp_size, tuple(blocks), heads, key.shape[0]
        ),
        out_shape=tuple(outs),
        in_specs=[ANY] * 3 + [VMEM] * 6,
        out_specs=(ANY,) * 3 + (VMEM,) * 4,
        scratch_shapes=[
            *LineGather.scratch(fsdp_size, shards, len(blocks)),
            pltpu.VMEM((heads * 128, width), LOW),
            pltpu.VMEM((half, width), WIDE),
            pltpu.VMEM((half, width), LOW),
            pltpu.VMEM((half, width), LOW),
            pltpu.VMEM((half, width), LOW),
            pltpu.VMEM((half, width), LOW),
            DMA((3,)),
            DMA((3,)),
            DMA((heads * HEAD_DIM // min(shards[0].shape[0], HEAD_DIM),)),
        ],
        compiler_params=pltpu.CompilerParams(
            collective_id=collective_id, has_side_effects=True, vmem_limit_bytes=50 * 2**20
        ),
    )(*shards, query, key, value, bias, hidden, gain)


class LineScatter:
    def __init__(self, ctx_size, fsdp_size, kinds, pieces, parts, outs, scratch):
        self.f, self.c, self.z, self.y, self.depth = place(fsdp_size)
        self.n = n = len(parts)
        self.kinds, self.pieces, self.parts, self.outs = kinds, pieces, parts, outs
        self.own, self.beside, self.far = scratch[:n], scratch[n : 2 * n], scratch[2 * n : 3 * n]
        self.cols = [w for w in range(n) if kinds[w] == "cols"]
        count = len(self.cols)
        rest = scratch[3 * n :]
        self.total, self.block, rest = rest[:count], rest[count : 2 * count], rest[2 * count :]
        self.local, self.y_send, self.y_recv, self.z_send, self.z_recv, *more = rest
        if count:
            self.c_send, self.c_recv = more
        self.order = []
        for t in range((self.depth + 1) // 2):
            ends = [self.depth - 1 - t, t]
            self.order += ends if ends[0] != t else [t]
        self.sequence = [(w, t) for w in range(n) for t in self.order]

    @staticmethod
    def shapes(ctx_size, parts, kinds, pieces):
        outs, chunks = [], []
        for part, kind, piece in zip(parts, kinds, pieces):
            if kind == "rows":
                chunks.append(part.shape[1:])
                outs.append(jax.ShapeDtypeStruct(part.shape[1:], WIDE))
                continue
            chunks.append((part.shape[0], *part.shape[2:]))
            rows = part.shape[2]
            for size, flat in piece:
                shape = (rows, ctx_size * size) if flat else (ctx_size, rows, size)
                outs.append(jax.ShapeDtypeStruct(shape, WIDE))
        return outs, chunks

    @staticmethod
    def scratch(fsdp_size, kinds, chunks):
        depth, n = fsdp_size // 2, len(chunks)
        wide = [chunk for chunk, kind in zip(chunks, kinds) if kind == "cols"]
        shapes = [
            *[pltpu.VMEM((depth, *chunk), LOW) for chunk in chunks],
            *[pltpu.VMEM((depth, *chunk), LOW) for chunk in chunks],
            *[pltpu.VMEM((depth + 1, *chunk), LOW) for chunk in chunks],
            *[pltpu.VMEM(chunk, LOW) for chunk in wide],
            *[pltpu.VMEM((3, *chunk[1:]), LOW) for chunk in wide],
            DMA((n, depth)),
            DMA((n, depth)),
            DMA((n, depth)),
            DMA((n, depth)),
            DMA((n, depth + 1)),
        ]
        return shapes + ([DMA((len(wide), 3))] * 2 if wide else [])

    def chunk(self, w, row, column):
        at = row * 2 + column
        return self.parts[w].at[at] if self.kinds[w] == "rows" else self.parts[w].at[:, at]

    def y_copy(self, w, t):
        return remote(
            self.chunk(w, t, 1 - self.y),
            self.beside[w].at[t],
            self.y_send.at[w, t],
            self.y_recv.at[w, t],
            fsdp=self.f ^ 1,
        )

    def z_copy(self, w, t, step, slot):
        return remote(
            self.own[w].at[t],
            self.far[w].at[slot],
            self.z_send.at[w, t],
            self.z_recv.at[w, slot],
            fsdp=(self.z + step) * 2 + self.y,
        )

    def own_copy(self, w, t):
        return pltpu.make_async_copy(self.chunk(w, t, self.y), self.own[w].at[t], self.local.at[w, t])

    def c_copy(self, k, bits):
        return remote(
            self.total[k].at[self.c ^ bits],
            self.block[k].at[bits - 1],
            self.c_send.at[k, bits - 1],
            self.c_recv.at[k, bits - 1],
            ctx=self.c ^ bits,
        )

    def start(self):
        for w, t in self.sequence[:AHEAD]:
            self.y_copy(w, t).start()
        for w, t in self.sequence:
            self.own_copy(w, t).start()

    def step(self, index):
        w, t = self.sequence[index]
        own, beside, far = self.own[w], self.beside[w], self.far[w]
        self.own_copy(w, t).wait()
        self.y_copy(w, t).wait_recv()
        if index + AHEAD < len(self.sequence):
            self.y_copy(*self.sequence[index + AHEAD]).start()
        for step in (1, -1):
            ahead = (t - self.z) * step
            behind = (self.z - step >= 0) & (self.z - step < self.depth)

            @pl.when((ahead > 0) & behind)
            def _():
                self.z_copy(w, t, step, t).wait_recv()
                add_rows(own.at[t], (own.at[t], beside.at[t], far.at[t]))

            @pl.when((ahead > 0) & jnp.logical_not(behind))
            def _():
                add_rows(own.at[t], (own.at[t], beside.at[t]))

            slot = t if step == 1 else t + jnp.where(ahead == 1, self.depth - t, 0)

            @pl.when(ahead > 0)
            def _():
                self.z_copy(w, t, step, slot).start()

    def first_out(self, w):
        return sum(
            1 if self.kinds[v] == "rows" else len(self.pieces[v]) for v in range(w)
        )

    def settle(self, w):
        z, depth = self.z, self.depth
        pl.when(z > 0)(lambda: self.z_copy(w, 0, 1, z).wait_recv())
        pl.when(z < depth - 1)(lambda: self.z_copy(w, 0, 1, depth).wait_recv())
        rows = self.kinds[w] == "rows"
        target = self.outs[self.first_out(w)] if rows else self.total[self.cols.index(w)]
        home = [self.own[w].at[z], self.beside[w].at[z]]
        below, above = self.far[w].at[z], self.far[w].at[depth]
        pl.when(z == 0)(lambda: add_rows(target, (*home, above)))
        pl.when(z == depth - 1)(lambda: add_rows(target, (*home, below)))
        pl.when((z > 0) & (z < depth - 1))(lambda: add_rows(target, (*home, below, above)))
        if not rows:
            for bits in (1, 2, 3):
                self.c_copy(self.cols.index(w), bits).start()

    def spread(self, w):
        k, first = self.cols.index(w), self.first_out(w)
        for bits in (0, 1, 2, 3):
            if bits:
                self.c_copy(k, bits).wait_recv()
            source = self.total[k].at[self.c] if bits == 0 else self.block[k].at[bits - 1]
            at = 0
            for j, (size, flat) in enumerate(self.pieces[w]):
                value = source[:, at : at + size].astype(WIDE)
                if flat:
                    where = pl.ds(pl.multiple_of((self.c ^ bits) * size, 128), size)
                    self.outs[first + j][:, where] = value
                else:
                    self.outs[first + j][self.c ^ bits] = value
                at += size

    def steps(self):
        result = []
        for w in range(self.n):
            for i in range(self.depth):
                result.append(functools.partial(self.step, w * self.depth + i))
            if w:
                result.append(functools.partial(self.settle, w - 1))
        result.append(functools.partial(self.settle, self.n - 1))
        result += [functools.partial(self.spread, w) for w in self.cols]
        return result

    def finish(self):
        for w, t in self.sequence:
            self.y_copy(w, t).wait_send()
            for step in (1, -1):
                pl.when((t - self.z) * step > 0)(
                    lambda w=w, t=t, step=step: self.z_copy(w, t, step, t).wait_send()
                )
        for k in range(len(self.cols)):
            for bits in (1, 2, 3):
                self.c_copy(k, bits).wait_send()


def third_kernel(ctx_size, fsdp_size, kinds, pieces, n_out, heads, kv_heads, *refs):
    n = len(kinds)
    parts, refs = refs[:n], refs[n:]
    far_half, near_half, mid, gain, cot, w_full, refs = *refs[:6], refs[6:]
    query, key, value, bias, log, rows, refs = *refs[:6], refs[6:]
    outs, refs = refs[:n_out], refs[n_out:]
    grad_ffn, grad_mid, mid_low, grad_query, grad_key, grad_value, refs = *refs[:6], refs[6:]
    w_pad, core_in, pair, pair_in, grad_rows, c_send, c_recv, w_sem, *scratch = refs
    c = lax.axis_index("ctx")
    line = LineScatter(ctx_size, fsdp_size, kinds, pieces, parts, outs, scratch)
    tokens, half = query.shape[1], mid.shape[0]
    run_len, tile = half // 2, 128
    scale = HEAD_DIM**-0.5

    def exchange(index, src, dst, bits):
        return remote(src, dst, c_send.at[index], c_recv.at[index], ctx=c ^ bits)

    to_core = exchange(0, far_half, core_in, 1)
    to_x = exchange(1, pair, pair_in, 2)
    give = exchange(2, mid_low.at[pl.ds(0, half)], mid_low.at[pl.ds(half, half)], 1)
    shard = w_full.shape[1]
    piece = min(shard, HEAD_DIM)
    moves = []
    for at in range(0, heads * HEAD_DIM, piece):
        to = at // HEAD_DIM * 128 + at % HEAD_DIM
        src = w_full.at[at // shard, pl.ds(at % shard, piece)]
        moves.append(pltpu.make_async_copy(src, w_pad.at[pl.ds(to, piece)], w_sem.at[len(moves)]))

    def load_out():
        for move in moves:
            move.start()
        for h in range(heads):
            w_pad[pl.ds(h * 128 + HEAD_DIM, 128 - HEAD_DIM)] = jnp.zeros(
                (128 - HEAD_DIM, w_pad.shape[1]), LOW
            )

    def meet_core():
        to_core.wait_recv()
        add_rows(pair, (near_half, core_in))
        to_x.start()

    def meet_x():
        to_x.wait_recv()
        for block in (0, 1):

            def body(at, block=block):
                here = pl.ds(pl.multiple_of(at.start + block * run_len, 16), 16)
                there = pl.ds(pl.multiple_of(at.start + (1 - block) * run_len, 16), 16)
                grad = pair[here].astype(WIDE) + pair_in[there].astype(WIDE)
                grad_ffn[here] = grad
                recip = inverse_rms(mid[here])
                scaled = mid[here] * recip
                total = cot[here].astype(WIDE) + norm_backward(grad, scaled, recip, gain[0:1])
                grad_mid[here] = total
                mid_low[here] = total.astype(LOW)

            row_loop(run_len, body)
        give.start()

    def attend_back():
        for move in moves:
            move.wait()
        give.wait_recv()

        def back_out(at):
            grad_rows[at] = lax.dot_general(
                mid_low[at], w_pad[...], (((1,), (1,)), ((), ())), preferred_element_type=WIDE
            ).astype(LOW)

        row_loop(tokens, back_out, tile)
        grad_key[...] = jnp.zeros_like(grad_key)
        grad_value[...] = jnp.zeros_like(grad_value)

        def body(i, carry):
            h = i // (tokens // tile)
            r = i % (tokens // tile)
            at = pl.ds(pl.multiple_of(r * tile, tile), tile)
            lanes = pl.ds(pl.multiple_of(h * 128, 128), 128)
            g = h // (heads // kv_heads)
            q = query[h, at]
            s = lax.dot_general(
                q, key[g], (((1,), (1,)), ((), ())), preferred_element_type=WIDE
            )
            p = jnp.exp(s * scale + bias[at] - log[h, at])
            grad_out = grad_rows[at, lanes]
            delta = jnp.sum(
                grad_out.astype(WIDE) * rows[at, lanes].astype(WIDE), axis=-1, keepdims=True
            )
            grad_p = lax.dot_general(
                grad_out, value[g], (((1,), (1,)), ((), ())), preferred_element_type=WIDE
            )
            grad_s = (p * (grad_p - delta)).astype(LOW)
            grad_query[h, at] = jnp.dot(grad_s, key[g], preferred_element_type=WIDE) * scale
            grad_key[g] = grad_key[g] + contract_rows(grad_s, q)
            grad_value[g] = grad_value[g] + contract_rows(p.astype(LOW), grad_out)
            return carry

        lax.fori_loop(0, heads * (tokens // tile), body, 0)
        grad_key[...] = grad_key[...] * scale

    greet(fsdp_size)
    to_core.start()
    line.start()
    inserts = {
        0: [load_out, meet_core],
        1: [meet_x],
        2: [attend_back],
    }
    weave(line.steps(), inserts)
    line.finish()
    for copy in (to_core, to_x, give):
        copy.wait_send()


def scatter_third(ctx_size, fsdp_size, collective_id, parts, kinds, pieces, small):
    outs, chunks = LineScatter.shapes(ctx_size, parts, kinds, pieces)
    n_out = len(outs)
    far_half, near_half, mid, gain, cot, w_full, query, key = small[:8]
    half, width = mid.shape
    heads, tokens, _ = query.shape
    kv_heads = key.shape[0]
    outs += [
        jax.ShapeDtypeStruct((half, width), WIDE),
        jax.ShapeDtypeStruct((half, width), WIDE),
        jax.ShapeDtypeStruct((tokens, width), LOW),
        jax.ShapeDtypeStruct(query.shape, WIDE),
        jax.ShapeDtypeStruct(key.shape, WIDE),
        jax.ShapeDtypeStruct(key.shape, WIDE),
    ]
    results = pl.pallas_call(
        functools.partial(
            third_kernel, ctx_size, fsdp_size, kinds, pieces, n_out, heads, kv_heads
        ),
        out_shape=tuple(outs),
        in_specs=[ANY] * len(parts) + [VMEM] * 5 + [ANY] + [VMEM] * 6,
        out_specs=(VMEM,) * len(outs),
        scratch_shapes=[
            pltpu.VMEM((heads * 128, width), LOW),
            pltpu.VMEM((half, width), LOW),
            pltpu.VMEM((half, width), LOW),
            pltpu.VMEM((half, width), LOW),
            pltpu.VMEM((tokens, heads * 128), LOW),
            DMA((3,)),
            DMA((3,)),
            DMA((heads * HEAD_DIM // min(w_full.shape[1], HEAD_DIM),)),
            *LineScatter.scratch(fsdp_size, kinds, chunks),
        ],
        compiler_params=pltpu.CompilerParams(
            collective_id=collective_id, has_side_effects=True, vmem_limit_bytes=58 * 2**20
        ),
    )(*parts, *small)
    return results[:n_out], results[n_out:]


def last_kernel(ctx_size, fsdp_size, kinds, pieces, n_out, *refs):
    n = len(kinds)
    parts, refs = refs[:n], refs[n:]
    out_far, out_near, in_far, in_near, mid, grad_mid, hidden, gain, grad_ffn, refs = (
        *refs[:9],
        refs[9:],
    )
    outs, refs = refs[:n_out], refs[n_out:]
    output, grad_in, gain_out, refs = *refs[:3], refs[3:]
    core_in, swap_out, swap_in, gain_own, gain_in, c_send, c_recv, g_send, g_recv, *scratch = refs
    line = LineScatter(ctx_size, fsdp_size, kinds, pieces, parts, outs, scratch)
    f, c, z, y, depth = place(fsdp_size)
    half = out_near.shape[0]
    run_len = half // 2

    def exchange(index, src, dst, bits):
        return remote(src, dst, c_send.at[index], c_recv.at[index], ctx=c ^ bits)

    cores = [exchange(0, in_far, core_in.at[0], 1), exchange(1, out_far, core_in.at[1], 1)]
    swaps = [exchange(2 + i, swap_out.at[i], swap_in.at[i], 2) for i in (0, 1)]
    near = (in_near, out_near)

    def meet_core(i):
        cores[i].wait_recv()

        def body(at):
            there = pl.ds(pl.multiple_of(at.start + run_len, 16), 16)
            swap_out[i, at] = (near[i][there] + core_in[i, there].astype(WIDE)).astype(LOW)

        row_loop(run_len, body)
        swaps[i].start()

    def own_sum(i, at):
        return near[i][at] + core_in[i, at].astype(WIDE) + swap_in[i, at].astype(WIDE)

    def meet_in():
        swaps[0].wait_recv()
        gain_own[...] = jnp.zeros_like(gain_own)

        def body(at):
            grad = own_sum(0, at)
            values = hidden[at].astype(WIDE)
            recip = inverse_rms(values)
            scaled = values * recip
            grad_in[at] = grad_mid[at] + norm_backward(grad, scaled, recip, gain[0:1])
            gain_own[0, 0:1] = gain_own[0, 0:1] + jnp.sum(grad * scaled, axis=0, keepdims=True)
            mids = mid[at]
            gain_own[0, 1:2] = gain_own[0, 1:2] + jnp.sum(
                grad_ffn[at] * (mids * inverse_rms(mids)), axis=0, keepdims=True
            )

        row_loop(run_len, body)

    def meet_out():
        swaps[1].wait_recv()

        def body(at):
            output[at] = (mid[at] + own_sum(1, at)).astype(LOW)

        row_loop(run_len, body)

    def gain_copy(i):
        where = ({"ctx": c ^ 1}, {"ctx": c ^ 2}, {"fsdp": f ^ 1})[i]
        return remote(gain_own.at[i], gain_in.at[i], g_send.at[i], g_recv.at[i], **where)

    def gain_meet(i):
        if i:
            gain_copy(i - 1).wait_recv()
            gain_own[i] = gain_own[i - 1] + gain_in[i - 1]
        gain_copy(i).start()

    gain_far = 3

    def up_copy():
        return remote(
            gain_own.at[4], gain_in.at[gain_far], g_send.at[3], g_recv.at[3], fsdp=(z + 1) * 2 + y
        )

    def down_copy():
        return remote(
            gain_own.at[5],
            gain_in.at[gain_far + 1],
            g_send.at[4],
            g_recv.at[4],
            fsdp=(z - 1) * 2 + y,
        )

    def gain_line():
        gain_copy(2).wait_recv()
        gain_own[3] = gain_own[2] + gain_in[2]

        @pl.when(z > 0)
        def _():
            remote(
                gain_own.at[4], gain_in.at[gain_far], g_send.at[3], g_recv.at[3], ctx=c ^ 1
            ).wait_recv()
            gain_own[4] = gain_own[3] + gain_in[gain_far]

        @pl.when(z == 0)
        def _():
            gain_own[4] = gain_own[3]

        pl.when(z + 1 < depth)(lambda: up_copy().start())

        @pl.when(z + 1 < depth)
        def _():
            remote(
                gain_own.at[5], gain_in.at[gain_far + 1], g_send.at[4], g_recv.at[4], ctx=c ^ 1
            ).wait_recv()
            gain_own[5] = gain_own[3] + gain_in[gain_far + 1]

        @pl.when(z + 1 == depth)
        def _():
            gain_own[5] = gain_own[3]

        pl.when(z > 0)(lambda: down_copy().start())
        gain_out[...] = gain_own[4] + gain_own[5] - gain_own[3]

    greet(fsdp_size)
    for copy in cores:
        copy.start()
    line.start()
    steps = line.steps()
    inserts = {
        0: [lambda: meet_core(0), lambda: meet_core(1)],
        2: [meet_in, lambda: gain_meet(0)],
        3: [lambda: gain_meet(1), meet_out],
        4: [lambda: gain_meet(2)],
        5: [gain_line],
    }
    weave(steps, inserts)
    line.finish()
    for copy in (*cores, *swaps, gain_copy(0), gain_copy(1), gain_copy(2)):
        copy.wait_send()
    pl.when(z + 1 < depth)(lambda: up_copy().wait_send())
    pl.when(z > 0)(lambda: down_copy().wait_send())


def scatter_last(ctx_size, fsdp_size, collective_id, parts, kinds, pieces, small):
    outs, chunks = LineScatter.shapes(ctx_size, parts, kinds, pieces)
    n_out = len(outs)
    half, width = small[0].shape
    run_len = half // 2
    outs += [
        jax.ShapeDtypeStruct((run_len, width), LOW),
        jax.ShapeDtypeStruct((run_len, width), WIDE),
        jax.ShapeDtypeStruct((8, width), WIDE),
    ]
    results = pl.pallas_call(
        functools.partial(last_kernel, ctx_size, fsdp_size, kinds, pieces, n_out),
        out_shape=tuple(outs),
        in_specs=[ANY] * len(parts) + [VMEM] * 9,
        out_specs=(VMEM,) * len(outs),
        scratch_shapes=[
            pltpu.VMEM((2, half, width), LOW),
            pltpu.VMEM((2, run_len, width), LOW),
            pltpu.VMEM((2, run_len, width), LOW),
            pltpu.VMEM((6, 8, width), WIDE),
            pltpu.VMEM((5, 8, width), WIDE),
            DMA((4,)),
            DMA((4,)),
            DMA((5,)),
            DMA((5,)),
            *LineScatter.scratch(fsdp_size, kinds, chunks),
        ],
        compiler_params=pltpu.CompilerParams(
            collective_id=collective_id, has_side_effects=True, vmem_limit_bytes=50 * 2**20
        ),
    )(*parts, *small)
    return results[:n_out], results[n_out:]


def inverse_rms(values):
    return lax.rsqrt(jnp.mean(values * values, axis=-1, keepdims=True) + EPS)


def norm_backward(grad_normed, scaled, inv_rms, gain):
    grad_scaled = grad_normed * gain
    return inv_rms * (
        grad_scaled - scaled * jnp.mean(grad_scaled * scaled, axis=-1, keepdims=True)
    )


def rope_tables(positions):
    half_dim = HEAD_DIM // 2
    freq_index = jnp.arange(half_dim, dtype=jnp.float32)
    frequency = jnp.exp(freq_index * (-2.0 / HEAD_DIM) * math.log(ROPE_BASE))
    angles = positions.astype(jnp.float32)[:, None] * frequency
    return (jnp.cos(angles)[:, None, :], jnp.sin(angles)[:, None, :])


def rotate(tensor, cosine, sine):
    half_dim = tensor.shape[-1] // 2
    front, back = tensor[..., :half_dim], tensor[..., half_dim:]
    return jnp.concatenate([front * cosine - back * sine, back * cosine + front * sine], axis=-1)


def rotate_back(tensor, cosine, sine):
    return rotate(tensor, cosine, -sine)


def dot(left, right):
    return jnp.dot(left, right, preferred_element_type=jnp.float32)


def contract_rows(left, right):
    return lax.dot_general(
        left, right, (((0,), (0,)), ((), ())), preferred_element_type=jnp.float32
    )


def times_transpose(left, weight):
    return lax.dot_general(
        left, weight, (((1,), (1,)), ((), ())), preferred_element_type=jnp.float32
    )


def make_step(ctx_size, fsdp_size):
    def per_device(
        hidden_in,
        segments,
        w_query,
        w_key,
        w_value,
        w_out,
        w_gate,
        w_up,
        w_down,
        attn_gain,
        ffn_gain,
        grad_out,
    ):
        _, run_len, width = hidden_in.shape
        c_index, f_index = lax.axis_index("ctx"), lax.axis_index("fsdp")
        heads, kv_heads = HEADS // ctx_size, KV_HEADS // ctx_size
        q_cols, kv_cols = heads * HEAD_DIM, kv_heads * HEAD_DIM
        ff = w_gate.shape[1] // ctx_size
        shard = width // fsdp_size
        owned = shard // ctx_size
        half = 2 * run_len

        def columns(weight, size):
            return lax.dynamic_slice_in_dim(weight, c_index * size, size, 1)

        own_hidden = hidden_in.reshape(run_len, width)
        blocks, (hidden, cotangent, seg_rows) = gather_first(
            ctx_size,
            fsdp_size,
            0,
            (
                jnp.concatenate(
                    [columns(w_query, q_cols), columns(w_key, kv_cols), columns(w_value, kv_cols)],
                    axis=1,
                ),
                jnp.pad(jnp.stack([attn_gain, ffn_gain]), ((0, 6), (0, -shard % 128))),
            ),
            (own_hidden, grad_out.reshape(run_len, width), jnp.broadcast_to(segments, (8, run_len))),
        )
        full_qkv = blocks[0].reshape(width, q_cols + 2 * kv_cols)
        gains = jnp.swapaxes(blocks[1][:, :2, :shard], 0, 1).reshape(2, width).astype(WIDE)
        attn_gain_rows = jnp.broadcast_to(gains[:1], (8, width))
        ffn_gain_rows = jnp.broadcast_to(gains[1:], (8, width))
        hidden = hidden.reshape(-1, width)
        cotangent = cotangent.reshape(-1, width)

        seg_flat = seg_rows[:, 0].reshape(-1)
        runs = jnp.stack([c_index, c_index ^ 2, c_index ^ 1, c_index ^ 3])
        ids = (runs[:, None] * run_len + jnp.arange(run_len, dtype=jnp.int32)).reshape(-1)
        before = jnp.sum((seg_flat[None, :] < seg_flat[:, None]).astype(jnp.int32), axis=-1)
        cosine, sine = rope_tables(ids - before)
        allowed = (seg_flat[None, :] == seg_flat[:, None]) & (ids[None, :] <= ids[:, None])
        bias = jnp.where(allowed, 0.0, -1e30).astype(WIDE)
        tokens = ids.shape[0]

        def to_heads(tensor):
            padded = jnp.pad(tensor.astype(LOW), ((0, 0), (0, 0), (0, 128 - HEAD_DIM)))
            return jnp.swapaxes(padded, 0, 1)

        def from_heads(tensor):
            return jnp.swapaxes(tensor[:, :, :HEAD_DIM], 0, 1)

        hidden_wide = hidden.astype(WIDE)
        attn_normed = (hidden_wide * inverse_rms(hidden_wide) * gains[0]).astype(LOW)
        projected = dot(attn_normed, full_qkv)
        query = projected[:, :q_cols].reshape(tokens, heads, HEAD_DIM)
        key = projected[:, q_cols : q_cols + kv_cols].reshape(tokens, kv_heads, HEAD_DIM)
        value = projected[:, q_cols + kv_cols :].reshape(tokens, kv_heads, HEAD_DIM)
        query = to_heads(rotate(query, cosine, sine))
        key = to_heads(rotate(key, cosine, sine))
        value = to_heads(value)

        gate_up_shard = jnp.concatenate([columns(w_gate, ff), columns(w_up, ff)], axis=1)
        full_out, full_gate_up, full_down, attn_rows, log_total, mid, ffn_normed = gather_second(
            ctx_size,
            fsdp_size,
            1,
            (w_out, gate_up_shard, w_down),
            query,
            key,
            value,
            bias,
            hidden[:half],
            ffn_gain_rows,
        )
        full_gate_up = full_gate_up.reshape(width, 2 * ff)
        full_down = full_down.reshape(ff, width)

        gate_up = dot(ffn_normed, full_gate_up)
        gate, up = gate_up[:, :ff], gate_up[:, ff:]
        sigmoid = jax.nn.sigmoid(gate)
        silu = gate * sigmoid
        inner = (silu * up).astype(LOW)
        part_output = dot(inner, full_down)
        part_down = contract_rows(inner, cotangent).astype(LOW)
        grad_inner = times_transpose(cotangent, full_down)
        grad_gate = grad_inner * up * sigmoid * (1.0 + gate * (1.0 - sigmoid))
        grad_gate_up = jnp.concatenate(
            [grad_gate.astype(LOW), (grad_inner * silu).astype(LOW)], axis=1
        )
        part_ffn = times_transpose(grad_gate_up, full_gate_up)
        part_gate_up = contract_rows(ffn_normed, grad_gate_up).astype(LOW)

        (grad_gate_w, grad_up_w, grad_down_w), back = scatter_third(
            ctx_size,
            fsdp_size,
            2,
            (
                part_gate_up.reshape(ctx_size, fsdp_size, owned, 2 * ff),
                part_down.reshape(fsdp_size, -1, width),
            ),
            ("cols", "rows"),
            (((ff, True), (ff, True)), None),
            (
                part_ffn[half:].astype(LOW),
                part_ffn[:half],
                mid,
                ffn_gain_rows,
                cotangent[:half],
                full_out,
                query,
                key,
                value,
                bias,
                log_total,
                attn_rows,
            ),
        )
        grad_ffn, grad_mid, grad_mid_low, grad_query, grad_key, grad_value = back

        grad_qkv = jnp.concatenate(
            [
                rotate_back(from_heads(grad_query), cosine, sine).astype(LOW).reshape(tokens, -1),
                rotate_back(from_heads(grad_key), cosine, sine).astype(LOW).reshape(tokens, -1),
                from_heads(grad_value).astype(LOW).reshape(tokens, -1),
            ],
            axis=1,
        )
        part_qkv = contract_rows(attn_normed, grad_qkv).astype(LOW)
        part_out = contract_rows(attn_rows, grad_mid_low).astype(LOW)
        part_out = part_out.reshape(heads, 128, width)[:, :HEAD_DIM]
        part_in = times_transpose(grad_qkv, full_qkv)

        (grad_query_w, grad_kv_w, grad_out_w), (output, grad_in, gain_sums) = scatter_last(
            ctx_size,
            fsdp_size,
            3,
            (
                part_qkv.reshape(ctx_size, fsdp_size, owned, -1),
                part_out.reshape(fsdp_size, -1, width),
            ),
            ("cols", "rows"),
            (((q_cols, True), (2 * kv_cols, False)), None),
            (
                part_output[half:].astype(LOW),
                part_output[:half],
                part_in[half:].astype(LOW),
                part_in[:half],
                mid,
                grad_mid,
                own_hidden,
                attn_gain_rows,
                grad_ffn,
            ),
        )
        grad_kv_w = jnp.swapaxes(grad_kv_w, 0, 1)
        gain_own = lax.dynamic_slice_in_dim(
            gain_sums[:2], (c_index * fsdp_size + f_index) * owned, owned, 1
        )

        return (
            output[None],
            grad_in[None],
            grad_query_w,
            grad_kv_w[:, :, :kv_cols].reshape(owned, -1),
            grad_kv_w[:, :, kv_cols:].reshape(owned, -1),
            grad_out_w,
            grad_gate_w,
            grad_up_w,
            grad_down_w,
            gain_own[0],
            gain_own[1],
        )

    return per_device


def solution(mesh):
    rows = P("fsdp", None)
    spread = P(("ctx", "fsdp"), None)
    runs = P("fsdp", "ctx", None)
    return jax.shard_map(
        make_step(mesh.shape["ctx"], mesh.shape["fsdp"]),
        mesh=mesh,
        in_specs=(runs, P("fsdp", "ctx"), *[rows] * 7, P("fsdp"), P("fsdp"), runs),
        out_specs=(runs, runs, *[spread] * 7, P(("ctx", "fsdp")), P(("ctx", "fsdp"))),
        check_vma=False,
    )
```

profile of v0, /device:TPU:0, one launch (start us, length us, event | category | flops | bytes accessed | tf_op | source)
XLA Modules:
  0.0 472.5 jit_solution(3049424596705709925)
XLA Ops:
  2.8 1.2 broadcast_in_dim.41.refs_4_
  4.1 1.1 constant_dynamic-slice_fusion.3
  5.2 0.8 pad_maximum_fusion.8.refs_0_
  6.0 1.2 constant_dynamic-slice_fusion.1
  7.3 40.8 %shard_map.203 = (bf16[8,192,768]{2,1,0:T(8,128)(2,1)}, bf16[8,8,256]{2,1,0:T(8,128)(2,1)}, bf16[4,128,1536]{2,1,0:T(8,128)(2,1)}, bf16[4,128,1536]{2,1,0:T(8,128)(2,1)}, s32[4,8,128]{2,1,0:T(8,128)}) custom-call(bf16[192,768]{1,0:T(8,128)(2,1)} %pad_maximum_fusion.8.refs_0_, bf16[8,256]{1,0:T(8,128)(2,1)} %fusion.20.refs_1_, bf16[128,1536]{1,0:T(8,128)(2,1)} %bitcast.76, ...), custom_call_target="tpu_custom_call" | custom-call | tf_op jit(solution)/shard_map/pallas_call | solution.py:290
  48.1 0.9 convert_bitcast_fusion
  50.1 1.8 multiply_reduce_fusion
  52.1 1.8 fusion.14
  53.8 0.9 slice.133
  54.8 1.3 and_select_fusion.refs_6_.refs_11_
  56.6 1.7 fusion.1
  58.8 1.4 fusion.29
  60.2 1.1 copy-done.12
  61.9 2.0 slice.156
  63.8 1.2 slice.153
  65.0 2.0 copy.26
  67.0 1.1 copy.23
  68.1 2.1 fusion.26
  70.2 1.7 fusion.27
  71.9 1.1 copy.39
  73.1 1.0 copy.38
  74.1 1.2 subtract_convert_fusion.3
  75.5 2.4 copy.37
  77.9 1.3 copy.36
  79.2 1.9 subtract_convert_fusion.1
  81.5 118.2 %shard_map.204 = (bf16[2,192,1536]{2,1,0:T(8,128)(2,1)}, bf16[8,192,2048]{2,1,0:T(8,128)(2,1)}, bf16[2,512,1536]{2,1,0:T(8,128)(2,1)}, bf16[512,512]{1,0:T(8,128...) custom-call(bf16[192,1536]{1,0:T(8,128)(2,1)S(1)} %copy-done.6, ...), custom_call_target="tpu_custom_call" | custom-call | tf_op jit(solution)/shard_map/pallas_call | solution.py:437
  199.8 6.2 %fusion.30 = f32[512,2048]{1,0:T(8,128)S(1)} fusion(bf16[512,1536]{1,0:T(8,128)(2,1)} %get-tuple-element.42, bf16[1536,2048]{1,0:T(8,128)(2,1)} %bitcast.103), kind=kOutput, calls=%fused_computation.87 | convolution fusion | flops 3221225472 | bytes 12058624 | tf_op jit(solution)/shard_map/dot_general | solution.py:995
  206.0 2.6 multiply_convert_fusion.3
  208.6 1.8 fusion.31
  210.4 3.5 fusion.3
  213.9 1.0 slice.209.refs_2_
  214.9 1.3 slice.164.refs_3_
  216.2 1.2 slice.172.refs_3_
  217.5 3.6 convolution_convert_fusion.1
  221.1 5.5 %convolution_convert_fusion = bf16[1536,2048]{1,0:T(8,128)(2,1)} fusion(bf16[512,1536]{1,0:T(8,128)(2,1)S(1)} %copy-done.25, bf16[512,1024]{1,0:T(8,128)(2,1)S(1)} %get-tuple-element.68, bf16[512,1024]{1,0:T(8,128)(2,1)S(1)} %get-tuple-element.67), kind=kOutput, calls=%fused_computation | convolution fusion | flops 3228565504 | bytes 9961472 | tf_op jit(solution)/shard_map/dot_general | solution.py:999
  226.6 147.3 %shard_map.205 = (f32[48,4096]{1,0:T(8,128)}, f32[48,4096]{1,0:T(8,128)}, f32[128,1536]{1,0:T(8,128)}, f32[256,1536]{1,0:T(8,128)}, f32[256,1536]{1,0:T(8,128)},...) custom-call(bf16[4,8,48,2048]{3,2,1,0:T(8,128)(2,1)} %bitcast.81, ...), custom_call_target="tpu_custom_call" | custom-call | tf_op jit(solution)/shard_map/pallas_call | solution.py:768
  373.9 1.3 slice_bitcast_fusion
  377.5 3.2 fusion.10
  380.8 2.9 convolution_convert_fusion.2
  383.7 1.3 slice.174.refs_5_
  385.8 1.0 convolution_convert_fusion.3
  386.8 1.2 slice.170
  388.0 76.2 %shard_map.206 = (f32[48,1536]{1,0:T(8,128)S(1)}, f32[4,48,384]{2,1,0:T(8,128)S(1)}, f32[48,1536]{1,0:T(8,128)S(1)}, bf16[128,1536]{1,0:T(8,128)(2,1)S(1)}, f32[...) custom-call(bf16[4,8,48,768]{3,2,1,0:T(8,128)(2,1)} %bitcast.86, bf16[8,48,1536]{2,1,0:T(8,128)(2,1)} %bitcast.82, ...), custom_call_target="tpu_custom_call" | custom-call | tf_op jit(solution)/shard_map/pallas_call | solution.py:941
  465.0 0.8 reshape.284
  467.5 0.9 copy.48
  469.8 0.9 copy.51
  470.7 0.9 copy.52
  471.6 0.9 copy.53
  (102 shorter events, 12.8 us)
Async XLA Ops:
  0.6 3.4 copy-start
  48.1 5.7 %copy-start.19 = (bf16[4,128,1536]{2,1,0:T(8,128)(2,1)S(1)}, bf16[4,128,1536]{2,1,0:T(8,128)(2,1)}, u32[]{:S(2)}) copy-start(bf16[4,128,1536]{2,1,0:T(8,128)(2,1)} %get-tuple-element.43) | copy-start | bytes 4718596
  52.0 2.7 copy-start.10
  52.0 29.5 %copy-start.9 = (f32[8,1536]{1,0:T(8,128)}, f32[8,1536]{1,0:T(8,128)S(1)}, u32[]{:S(2)}) copy-start(f32[8,1536]{1,0:T(8,128)S(1)} %broadcast_in_dim.45.refs_8_.refs_5_) | copy-start | bytes 147460
  56.6 2.2 copy-start.23
  60.2 1.2 copy-start.12
  61.8 19.7 %copy-start.4 = (bf16[2,512,128]{2,1,0:T(8,128)(2,1)}, bf16[2,512,128]{2,1,0:T(8,128)(2,1)S(1)}, u32[]{:S(2)}) copy-start(bf16[2,512,128]{2,1,0:T(8,128)(2,1)S(1)} %pad_bitcast_fusion.refs_5_.refs_10_) | copy-start | bytes 786436
  68.1 5.9 %copy-start.11 = (f32[512,48]{1,0:T(8,128)S(1)}, f32[512,48]{1,0:T(8,128)}, u32[]{:S(2)}) copy-start(f32[512,48]{1,0:T(8,128)} %get-tuple-element.85) | copy-start | bytes 294916
  75.3 2.6 copy-start.14
  75.5 6.0 %copy-start.3 = (bf16[2,512,128]{2,1,0:T(8,128)(2,1)}, bf16[2,512,128]{2,1,0:T(8,128)(2,1)S(1)}, u32[]{:S(2)}) copy-start(bf16[2,512,128]{2,1,0:T(8,128)(2,1)S(1)} %fusion.12.refs_4_.refs_9_) | copy-start | bytes 786436
  79.2 2.3 copy-start.6
  81.5 118.2 %copy-start.2 = (bf16[4,512,128]{2,1,0:T(8,128)(2,1)}, bf16[4,512,128]{2,1,0:T(8,128)(2,1)S(1)}, u32[]{:S(2)}) copy-start(bf16[4,512,128]{2,1,0:T(8,128)(2,1)S(1)} %fusion.7.refs_3_.refs_8_) | copy-start | bytes 1572868
  199.7 6.2 %copy-start.7 = (bf16[512,512]{1,0:T(8,128)(2,1)}, bf16[512,512]{1,0:T(8,128)(2,1)S(1)}, u32[]{:S(2)}) copy-start(bf16[512,512]{1,0:T(8,128)(2,1)S(1)} %get-tuple-element.49.refs_13_) | copy-start | bytes 1572868
  199.7 6.2 %copy-start.20 = (bf16[4,128,1536]{2,1,0:T(8,128)(2,1)S(1)}, bf16[4,128,1536]{2,1,0:T(8,128)(2,1)}, u32[]{:S(2)}) copy-start(bf16[4,128,1536]{2,1,0:T(8,128)(2,1)} %get-tuple-element.43) | copy-start | bytes 4718596
  199.7 6.2 %copy-start.22 = (bf16[2,512,1536]{2,1,0:T(8,128)(2,1)S(1)}, bf16[2,512,1536]{2,1,0:T(8,128)(2,1)}, u32[]{:S(2)}) copy-start(bf16[2,512,1536]{2,1,0:T(8,128)(2,1)} %get-tuple-element.44) | copy-start | bytes 9437188
  199.7 10.7 %slice-start = ((s8[6291456]{0:T(1024)(128)(4,1)}), s8[4194304]{0:T(1024)(128)(4,1)S(1)}, s32[]{:S(2)}) async-start(s8[6291456]{0:T(1024)(128)(4,1)} %bitcast.104), calls=%async_computation | async-start | bytes 8388608
  206.0 4.4 slice-start.1
  217.5 3.6 copy-start.25
  375.7 1.0 copy-start.21
  375.7 1.2 copy-start.18
  377.5 3.2 copy-start.13
  383.6 1.4 copy-start.8
  383.6 2.1 copy-start.24
  386.8 1.2 copy-start.5
  465.8 4.0 copy-start.17
  467.5 3.2 copy-start.16
  468.4 3.2 copy-start.15
  469.1 3.4 copy-start.1
where the time goes:
time: 477 us; the launch traced here: 472 us
  Pallas kernels  382 us (80%)
  local copies, waits for them, and re-layouts  42.6 us (9%)
  matrix products  31.6 us (7%)
  other arithmetic  14.5 us (3%)
    pallas_call x1, Pallas kernels, scatter_third(): pl.pallas_call(functools.partial(third_kernel, ctx_size, fsdp_size, kinds...  147 us
    pallas_call x1, Pallas kernels, gather_second(): pl.pallas_call(functools.partial(second_kernel, ctx_size, fsdp_size, tupl...  118 us
    pallas_call x1, Pallas kernels, scatter_last(): pl.pallas_call(functools.partial(last_kernel, ctx_size, fsdp_size, kinds,...  76.2 us
    pallas_call x1, Pallas kernels, gather_first(): pl.pallas_call(functools.partial(first_kernel, ctx_size, fsdp_size, n_blo...  40.8 us
    unnamed x67, local copies, waits for them, and re-layouts  14.7 us
    dot_general x4, matrix products, contract_rows(): lax.dot_general(left, right, (((0,), (0,)), ((), ())), preferred_element_...  13 us

commit v1 on v0

v1 whole, which is shorter than its diff:
```python
import functools
import math

import jax
import jax.numpy as jnp
from jax import lax
from jax.experimental import pallas as pl
from jax.experimental.pallas import tpu as pltpu
from jax.sharding import PartitionSpec as P

HEADS = 16
KV_HEADS = 8
HEAD_DIM = 96
EPS = 1e-05
ROPE_BASE = 100000.0

AHEAD = 4
MESH = pl.DeviceIdType.MESH
ANY = pl.BlockSpec(memory_space=pl.ANY)
VMEM = pl.BlockSpec(memory_space=pltpu.VMEM)
DMA = pltpu.SemaphoreType.DMA
LOW = jnp.bfloat16
WIDE = jnp.float32


def remote(src, dst, send, recv, **where):
    return pltpu.make_async_remote_copy(
        src_ref=src,
        dst_ref=dst,
        send_sem=send,
        recv_sem=recv,
        device_id=where,
        device_id_type=MESH,
    )


def place(fsdp_size):
    f, c = lax.axis_index("fsdp"), lax.axis_index("ctx")
    return f, c, f // 2, f % 2, fsdp_size // 2


def greet(fsdp_size, all_rows=False):
    f, c, z, y, depth = place(fsdp_size)
    barrier = pltpu.get_barrier_semaphore()
    for bits in (1, 2, 3):
        pl.semaphore_signal(barrier, inc=1, device_id={"ctx": c ^ bits}, device_id_type=MESH)
    pl.semaphore_signal(barrier, inc=1, device_id={"fsdp": f ^ 1}, device_id_type=MESH)
    if all_rows:
        for shift in range(1, depth):
            row = (z + shift) % depth
            pl.semaphore_signal(
                barrier, inc=1, device_id={"fsdp": row * 2 + y}, device_id_type=MESH
            )
        pl.semaphore_wait(barrier, depth + 3)
        return
    for step in (1, -1):
        near = z + step

        @pl.when((near >= 0) & (near < depth))
        def _():
            pl.semaphore_signal(
                barrier, inc=1, device_id={"fsdp": near * 2 + y}, device_id_type=MESH
            )

    pl.semaphore_wait(barrier, 4 + jnp.minimum(z, 1) + jnp.minimum(depth - 1 - z, 1))


class LineGather:
    def __init__(self, ctx_size, fsdp_size, masked, blocks, owns, fulls, stages, sems):
        self.sizes = ctx_size, fsdp_size
        self.f, self.c, self.z, self.y, self.depth = place(fsdp_size)
        self.masked, self.blocks = masked, blocks
        self.owns, self.fulls, self.stages = owns, fulls, stages
        self.z_send, self.z_recv, self.y_send, self.y_recv, self.local = sems
        self.beside_done = set()

    @staticmethod
    def scratch(fsdp_size, arrays, count):
        depth = fsdp_size // 2
        return [
            *[pltpu.VMEM(a.shape, a.dtype) for a in arrays],
            DMA((count, 2, depth - 1)),
            DMA((count, 2, depth - 1)),
            DMA((count, 2 * depth - 1)),
            DMA((count, 2 * depth - 1)),
            DMA((len(arrays),)),
        ]

    def held(self, a, row):
        there = (row >= 0) & (row < self.depth)
        if self.masked[a]:
            span = self.depth // self.sizes[0]
            there = there & (row >= self.c * span) & (row < (self.c + 1) * span)
        return there

    def entry(self, a, row, column):
        base = self.c * (self.sizes[1] // self.sizes[0]) if self.masked[a] else 0
        return row * 2 + column - base

    def spot(self, b, row, column):
        a, low, size = self.blocks[b]
        return self.fulls[a].at[self.entry(a, row, column), pl.ds(low, size)]

    def source(self, b, row):
        a, low, size = self.blocks[b]
        return self.owns[a].at[pl.ds(low, size)] if row is None else self.spot(b, row, self.y)

    def z_copy(self, b, way, hop):
        step = 1 if way == 0 else -1
        row = self.z - step * (hop - 1)
        near = self.z + step
        copy = remote(
            self.source(b, None if hop == 1 else row),
            self.spot(b, row, self.y),
            self.z_send.at[b, way, hop - 1],
            self.z_recv.at[b, way, hop - 1],
            fsdp=near * 2 + self.y,
        )
        return copy, self.held(self.blocks[b][0], row) & (near >= 0) & (near < self.depth)

    def row_of(self, slot):
        return self.z - slot if slot < self.depth else self.z + (slot - self.depth + 1)

    def y_copy(self, b, slot):
        row = self.row_of(slot)
        copy = remote(
            self.source(b, row if slot else None),
            self.spot(b, row, self.y),
            self.y_send.at[b, slot],
            self.y_recv.at[b, slot],
            fsdp=self.f ^ 1,
        )
        return copy, self.held(self.blocks[b][0], row)

    @staticmethod
    def begin(pair):
        pl.when(pair[1])(lambda: pair[0].start())

    def send_own(self, b):
        self.begin(self.z_copy(b, 0, 1))
        self.begin(self.z_copy(b, 1, 1))
        self.begin(self.y_copy(b, 0))

    def local_in(self, a):
        return pltpu.make_async_copy(self.owns[a], self.stages[a], self.local.at[a])

    def local_out(self, a):
        spot = self.fulls[a].at[self.entry(a, self.z, self.y)]
        return pltpu.make_async_copy(self.stages[a], spot, self.local.at[a])

    def start(self):
        for a in range(len(self.owns)):
            self.local_in(a).start()
        for b in range(min(2, len(self.blocks))):
            self.send_own(b)
        for a in range(len(self.owns)):
            self.local_in(a).wait()
            pl.when(self.held(a, self.z))(lambda a=a: self.local_out(a).start())

    def step(self, b, hop):
        a = self.blocks[b][0]
        for way in (0, 1):
            row = self.z - hop if way == 0 else self.z + hop

            @pl.when(self.held(a, row))
            def _():
                remote(
                    self.source(b, None),
                    self.spot(b, row, self.y),
                    self.z_send.at[b, way, hop - 1],
                    self.z_recv.at[b, way, hop - 1],
                    fsdp=self.f ^ 1,
                ).wait_recv()

            if hop + 1 < self.depth:
                self.begin(self.z_copy(b, way, hop + 1))
            self.begin(self.y_copy(b, hop if way == 0 else self.depth - 1 + hop))
        if hop == 1 and b + 2 < len(self.blocks):
            self.send_own(b + 2)

    def steps(self):
        return [
            ((b, hop), functools.partial(self.step, b, hop))
            for b in range(len(self.blocks))
            for hop in range(1, self.depth)
        ]

    def wait_local(self, a):
        pl.when(self.held(a, self.z))(lambda: self.local_out(a).wait())

    def wait_beside(self, b):
        if b in self.beside_done:
            return
        self.beside_done.add(b)
        for slot in range(2 * self.depth - 1):
            row = self.row_of(slot)

            @pl.when(self.held(self.blocks[b][0], row))
            def _():
                remote(
                    self.source(b, None),
                    self.spot(b, row, 1 - self.y),
                    self.y_send.at[b, slot],
                    self.y_recv.at[b, slot],
                    fsdp=self.f ^ 1,
                ).wait_recv()

    def finish(self, local_done=()):
        for b in range(len(self.blocks)):
            self.wait_beside(b)
        pairs = []
        for b in range(len(self.blocks)):
            for hop in range(1, self.depth):
                pairs += [self.z_copy(b, 0, hop), self.z_copy(b, 1, hop)]
            pairs += [self.y_copy(b, slot) for slot in range(2 * self.depth - 1)]
        for copy, there in pairs:
            pl.when(there)(lambda copy=copy: copy.wait_send())
        for a in range(len(self.owns)):
            if a not in local_done:
                self.wait_local(a)


def weave(steps, inserts):
    for name, step in steps:
        for extra in inserts.pop(name, ()):
            extra()
        step()
    assert not inserts


def row_loop(total, body, rows=16):
    rows = rows if total % rows == 0 else total

    def run(step, carry):
        body(pl.ds(pl.multiple_of(step * rows, rows), rows))
        return carry

    lax.fori_loop(0, total // rows, run, 0)


def add_rows(out_ref, terms):
    shape = out_ref.shape
    leads = [None] if len(shape) == 2 else list(range(shape[0]))

    def body(at):
        for lead in leads:
            index = (at,) if lead is None else (lead, at)
            value = None
            for ref in terms:
                part = ref[index].astype(WIDE)
                value = part if value is None else value + part
            out_ref[index] = value.astype(out_ref.dtype)

    row_loop(shape[-2], body)


def front_kernel(ctx_size, fsdp_size, blocks, heads, kv_heads, *refs):
    owns, runs, frequency, refs = refs[:5], refs[5:9], refs[9], refs[10:]
    fulls, alls, refs = [None, *refs[:4]], refs[4:6], refs[6:]
    query, key, value, bias, cosine, sine, refs = *refs[:6], refs[6:]
    attn_normed, gains, rows_out, log_out, mid_out, normed, refs = *refs[:6], refs[6:]
    stages, sems, refs = refs[:5], refs[5:10], refs[10:]
    fulls[0], seg_rows, seg_cols, stage_runs, refs = refs[0], refs[1], refs[2], refs[3:5], refs[5:]
    select, w_proj, w_pad, kept, core_out, core_in, pair, pair_in, refs = *refs[:8], refs[8:]
    c_send, c_recv, r_send, r_recv, local, w_sem = refs
    c = lax.axis_index("ctx")
    masked = (False, False, True, False, True)
    line = LineGather(ctx_size, fsdp_size, masked, blocks, owns, fulls, stages, sems)
    hidden_all, cot_all = alls
    tokens = query.shape[1]
    run_len = tokens // ctx_size
    half = 2 * run_len
    scale = HEAD_DIM**-0.5
    tile = 128
    assert run_len == tile
    relation = (0, 2, 1, 3)

    targets = (seg_rows, seg_cols, hidden_all, cot_all)
    sources = (runs[2], runs[3], runs[0], runs[1])

    def run_copy(r, bits):
        return remote(
            sources[r],
            targets[r].at[relation[bits]],
            r_send.at[r, bits - 1],
            r_recv.at[r, bits - 1],
            ctx=c ^ bits,
        )

    def run_in(r):
        dst = targets[r].at[0] if r < 3 else stage_runs[0]
        return pltpu.make_async_copy(sources[r], dst, local.at[r])

    def run_out():
        return pltpu.make_async_copy(stage_runs[0], cot_all.at[0], local.at[3])

    def start_runs():
        for r in (0, 1, 2, 3):
            run_in(r).start()
        for r in (0, 1, 2):
            for bits in (2, 1, 3):
                run_copy(r, bits).start()
        run_in(3).wait()
        run_out().start()

    def tables():
        for r in (0, 1, 2):
            run_in(r).wait()
            for bits in (2, 1, 3):
                run_copy(r, bits).wait_recv()
        for bits in (2, 1, 3):
            run_copy(3, bits).start()
        down = lax.broadcasted_iota(jnp.int32, (tile, tile), 0)
        across = lax.broadcasted_iota(jnp.int32, (tile, tile), 1)
        for r in range(ctx_size):
            at = pl.ds(r * tile, tile)
            own_seg = seg_cols[r]
            ids = (c ^ relation[r]) * tile + down
            before = jnp.zeros((tile, 1), WIDE)
            for k in range(ctx_size):
                other = seg_rows[k, 0:1]
                smaller = jnp.where(other < own_seg, 1.0, 0.0)
                before = before + jnp.sum(smaller, axis=-1, keepdims=True)
                seen = (other == own_seg) & ((c ^ relation[k]) * tile + across <= ids)
                bias[at, k * tile : (k + 1) * tile] = jnp.where(seen, 0.0, -1e30).astype(LOW)
            angles = (ids.astype(WIDE) - before) * frequency[0:1]
            cosine[at] = jnp.cos(angles)
            sine[at] = jnp.sin(angles)

    def first_norm():
        line.wait_beside(0)
        line.wait_local(0)
        shard = owns[1].shape[0]
        lanes = fulls[0].shape[-1]
        width = gains.shape[1]
        total = None
        for f in range(fsdp_size):
            wide = jnp.concatenate(
                [fulls[0][f], jnp.zeros((8, width - lanes), WIDE)], axis=1
            )
            wide = pltpu.roll(wide, f * shard, 1) if f else wide
            total = wide if total is None else total + wide
        gains[...] = total
        for r in range(ctx_size):

            def body(at, r=r):
                values = hidden_all[r, at].astype(WIDE)
                there = pl.ds(pl.multiple_of(at.start + r * run_len, 16), 16)
                attn_normed[there] = (values * inverse_rms(values) * gains[0:1]).astype(LOW)

            row_loop(run_len, body)

    def spread_weights():
        line.wait_beside(1)
        line.wait_local(1)
        shard = owns[1].shape[0]
        for f in range(fsdp_size):
            w_proj[f * shard : (f + 1) * shard] = jnp.dot(
                fulls[1][f], select[...], preferred_element_type=WIDE
            ).astype(LOW)

    def project_in():
        def body(at):
            for h in range(heads + 2 * kv_heads):
                lanes = pl.ds(h * 128, 128)
                tensor = jnp.dot(
                    attn_normed[at], w_proj[:, lanes], preferred_element_type=WIDE
                )
                if h < heads + kv_heads:
                    tensor = turn(tensor, cosine[at], sine[at])
                ref, g = (
                    (query, h)
                    if h < heads
                    else (key, h - heads)
                    if h < heads + kv_heads
                    else (value, h - heads - kv_heads)
                )
                ref[g, at] = tensor.astype(LOW)

        row_loop(tokens, body, tile)

    def attention(part):
        def body(i, carry):
            h = i // (tokens // tile)
            r = i % (tokens // tile)
            at = pl.ds(pl.multiple_of(r * tile, tile), tile)
            g = h // (heads // kv_heads)
            s = lax.dot_general(
                query[h, at], key[g], (((1,), (1,)), ((), ())), preferred_element_type=WIDE
            )
            s = s * scale + bias[at].astype(WIDE)
            top = jnp.max(s, axis=-1, keepdims=True)
            log = top + jnp.log(jnp.sum(jnp.exp(s - top), axis=-1, keepdims=True))
            p = jnp.exp(s - log).astype(LOW)
            mixed = jnp.dot(p, value[g], preferred_element_type=WIDE)
            rows_out[at, pl.ds(pl.multiple_of(h * 128, 128), 128)] = mixed.astype(LOW)
            log_out[h, at] = log
            return carry

        count = heads * (tokens // tile)
        lax.fori_loop(part * count // 2, (part + 1) * count // 2, body, 0)

    def exchange(index, src, dst, bits):
        return remote(src, dst, c_send.at[index], c_recv.at[index], ctx=c ^ bits)

    to_core = exchange(0, core_out, core_in, 1)
    to_x = exchange(1, pair, pair_in, 2)
    give = exchange(2, normed.at[pl.ds(0, half)], normed.at[pl.ds(half, half)], 1)

    shard = owns[2].shape[0]
    piece = min(shard, HEAD_DIM)
    moves = []
    for at in range(0, heads * HEAD_DIM, piece):
        to = at // HEAD_DIM * 128 + at % HEAD_DIM
        src = fulls[2].at[at // shard, pl.ds(at % shard, piece)]
        moves.append(pltpu.make_async_copy(src, w_pad.at[pl.ds(to, piece)], w_sem.at[len(moves)]))

    def load_out():
        line.wait_beside(2)
        line.wait_local(2)
        for move in moves:
            move.start()
        for h in range(heads):
            w_pad[pl.ds(h * 128 + HEAD_DIM, 128 - HEAD_DIM)] = jnp.zeros(
                (128 - HEAD_DIM, w_pad.shape[1]), LOW
            )
        for move in moves:
            move.wait()

    def project():
        def far(at):
            value_rows = rows_out[pl.ds(pl.multiple_of(at.start + half, tile), tile)]
            core_out[at] = jnp.dot(value_rows, w_pad[...], preferred_element_type=WIDE).astype(LOW)

        row_loop(half, far, tile)
        to_core.start()

        def near(at):
            kept[at] = jnp.dot(rows_out[at], w_pad[...], preferred_element_type=WIDE)

        row_loop(half, near, tile)

    def meet_core():
        to_core.wait_recv()
        add_rows(pair, (kept, core_in))
        to_x.start()

    def meet_x():
        to_x.wait_recv()
        for block in (0, 1):

            def body(at, block=block):
                here = pl.ds(pl.multiple_of(at.start + block * run_len, 16), 16)
                there = pl.ds(pl.multiple_of(at.start + (1 - block) * run_len, 16), 16)
                mid = hidden_all[block, at].astype(WIDE) + (
                    pair[here].astype(WIDE) + pair_in[there].astype(WIDE)
                )
                mid_out[here] = mid
                scaled = mid * inverse_rms(mid)
                normed[here] = (scaled * gains[1:2]).astype(LOW)

            row_loop(run_len, body)
        give.start()

    greet(fsdp_size)
    line.start()
    start_runs()
    fill_select(select)
    inserts = {
        (2, 1): [tables],
        (2, 2): [first_norm],
        (3, 1): [spread_weights],
        (3, 2): [project_in],
        (3, 3): [lambda: attention(0)],
        (4, 1): [lambda: attention(1)],
        (4, 2): [load_out, project],
        (4, 3): [meet_core],
        (6, 1): [meet_x],
    }
    weave(line.steps(), inserts)
    line.finish(local_done=(0, 1, 2))
    give.wait_recv()
    for copy in (to_core, to_x, give):
        copy.wait_send()
    for bits in (2, 1, 3):
        run_copy(3, bits).wait_recv()
        for r in (0, 1, 2, 3):
            run_copy(r, bits).wait_send()
    run_out().wait()


def gather_front(ctx_size, fsdp_size, collective_id, shards, runs, frequency, heads, kv_heads):
    run_len, width = runs[0].shape
    tokens, half = ctx_size * run_len, 2 * run_len
    few = fsdp_size // ctx_size
    counts = (fsdp_size, fsdp_size, few, fsdp_size, few)
    pieces = (1, 1, 1, 2, 4)
    blocks = []
    for a, shard in enumerate(shards):
        size = shard.shape[0] // pieces[a]
        blocks += [(a, i * size, size) for i in range(pieces[a])]
    fulls = [jax.ShapeDtypeStruct((n, *s.shape), s.dtype) for n, s in zip(counts, shards)]
    columns = shards[1].shape[1]
    padded = (heads + 2 * kv_heads) * 128
    outs = [
        *fulls[1:],
        jax.ShapeDtypeStruct((ctx_size, run_len, width), LOW),
        jax.ShapeDtypeStruct((ctx_size, run_len, width), LOW),
        jax.ShapeDtypeStruct((heads, tokens, 128), LOW),
        jax.ShapeDtypeStruct((kv_heads, tokens, 128), LOW),
        jax.ShapeDtypeStruct((kv_heads, tokens, 128), LOW),
        jax.ShapeDtypeStruct((tokens, tokens), LOW),
        jax.ShapeDtypeStruct((tokens, 128), WIDE),
        jax.ShapeDtypeStruct((tokens, 128), WIDE),
        jax.ShapeDtypeStruct((tokens, width), LOW),
        jax.ShapeDtypeStruct((8, width), WIDE),
        jax.ShapeDtypeStruct((tokens, heads * 128), LOW),
        jax.ShapeDtypeStruct((heads, tokens, 1), WIDE),
        jax.ShapeDtypeStruct((half, width), WIDE),
        jax.ShapeDtypeStruct((tokens, width), LOW),
    ]
    return pl.pallas_call(
        functools.partial(front_kernel, ctx_size, fsdp_size, tuple(blocks), heads, kv_heads),
        out_shape=tuple(outs),
        in_specs=[ANY] * 9 + [VMEM],
        out_specs=(VMEM, ANY, ANY, ANY, VMEM, ANY) + (VMEM,) * 12,
        scratch_shapes=[
            *LineGather.scratch(fsdp_size, shards, len(blocks)),
            pltpu.VMEM(fulls[0].shape, WIDE),
            pltpu.VMEM((ctx_size, *runs[2].shape), WIDE),
            pltpu.VMEM((ctx_size, *runs[3].shape), WIDE),
            pltpu.VMEM((run_len, width), LOW),
            pltpu.VMEM((8, 128), LOW),
            pltpu.VMEM((columns, padded), LOW),
            pltpu.VMEM((width, padded), LOW),
            pltpu.VMEM((heads * 128, width), LOW),
            pltpu.VMEM((half, width), WIDE),
            pltpu.VMEM((half, width), LOW),
            pltpu.VMEM((half, width), LOW),
            pltpu.VMEM((half, width), LOW),
            pltpu.VMEM((half, width), LOW),
            DMA((3,)),
            DMA((3,)),
            DMA((4, 3)),
            DMA((4, 3)),
            DMA((4,)),
            DMA((heads * HEAD_DIM // min(shards[2].shape[0], HEAD_DIM),)),
        ],
        compiler_params=pltpu.CompilerParams(
            collective_id=collective_id, has_side_effects=True, vmem_limit_bytes=58 * 2**20
        ),
    )(*shards, *runs, frequency)


class LineScatter:
    def __init__(self, ctx_size, fsdp_size, kinds, pieces, parts, outs, scratch):
        self.f, self.c, self.z, self.y, self.depth = place(fsdp_size)
        self.n = n = len(parts)
        self.kinds, self.pieces, self.parts, self.outs = kinds, pieces, parts, outs
        self.own, self.beside, self.far = scratch[:n], scratch[n : 2 * n], scratch[2 * n : 3 * n]
        self.cols = [w for w in range(n) if kinds[w] == "cols"]
        count = len(self.cols)
        rest = scratch[3 * n :]
        self.total, self.block, rest = rest[:count], rest[count : 2 * count], rest[2 * count :]
        self.local, self.y_send, self.y_recv, self.z_send, self.z_recv, *more = rest
        if count:
            self.c_send, self.c_recv = more
        self.order = []
        for t in range((self.depth + 1) // 2):
            ends = [self.depth - 1 - t, t]
            self.order += ends if ends[0] != t else [t]
        self.sequence = [(w, t) for w in range(n) for t in self.order]

    @staticmethod
    def shapes(ctx_size, parts, kinds, pieces):
        outs, chunks = [], []
        for part, kind, piece in zip(parts, kinds, pieces):
            if kind == "rows":
                chunks.append(part.shape[1:])
                outs.append(jax.ShapeDtypeStruct(part.shape[1:], WIDE))
                continue
            chunks.append((part.shape[0], *part.shape[2:]))
            rows = part.shape[2]
            for size, flat in piece:
                shape = (rows, ctx_size * size) if flat else (ctx_size, rows, size)
                outs.append(jax.ShapeDtypeStruct(shape, WIDE))
        return outs, chunks

    @staticmethod
    def scratch(fsdp_size, kinds, chunks):
        depth, n = fsdp_size // 2, len(chunks)
        wide = [chunk for chunk, kind in zip(chunks, kinds) if kind == "cols"]
        shapes = [
            *[pltpu.VMEM((depth, *chunk), LOW) for chunk in chunks],
            *[pltpu.VMEM((depth, *chunk), LOW) for chunk in chunks],
            *[pltpu.VMEM((depth + 1, *chunk), LOW) for chunk in chunks],
            *[pltpu.VMEM(chunk, LOW) for chunk in wide],
            *[pltpu.VMEM((3, *chunk[1:]), LOW) for chunk in wide],
            DMA((n, depth)),
            DMA((n, depth)),
            DMA((n, depth)),
            DMA((n, depth)),
            DMA((n, depth + 1)),
        ]
        return shapes + ([DMA((len(wide), 3))] * 2 if wide else [])

    def chunk(self, w, row, column):
        at = row * 2 + column
        return self.parts[w].at[at] if self.kinds[w] == "rows" else self.parts[w].at[:, at]

    def y_copy(self, w, t):
        return remote(
            self.chunk(w, t, 1 - self.y),
            self.beside[w].at[t],
            self.y_send.at[w, t],
            self.y_recv.at[w, t],
            fsdp=self.f ^ 1,
        )

    def z_copy(self, w, t, step, slot):
        return remote(
            self.own[w].at[t],
            self.far[w].at[slot],
            self.z_send.at[w, t],
            self.z_recv.at[w, slot],
            fsdp=(self.z + step) * 2 + self.y,
        )

    def own_copy(self, w, t):
        return pltpu.make_async_copy(self.chunk(w, t, self.y), self.own[w].at[t], self.local.at[w, t])

    def c_copy(self, k, bits):
        return remote(
            self.total[k].at[self.c ^ bits],
            self.block[k].at[bits - 1],
            self.c_send.at[k, bits - 1],
            self.c_recv.at[k, bits - 1],
            ctx=self.c ^ bits,
        )

    def start(self, ready):
        for w, t in self.sequence[:AHEAD]:
            self.y_copy(w, t).start()
        self.load(range(ready))

    def load(self, groups):
        for w in groups:
            for t in self.order:
                self.own_copy(w, t).start()

    def send_on(self, w, t, step, ahead):
        slot = t if step == 1 else t + jnp.where(ahead == 1, self.depth - t, 0)
        self.z_copy(w, t, step, slot).start()

    def near(self, index):
        w, t = self.sequence[index]
        own = self.own[w].at[t]
        self.own_copy(w, t).wait()
        self.y_copy(w, t).wait_recv()
        if index + AHEAD < len(self.sequence):
            self.y_copy(*self.sequence[index + AHEAD]).start()
        for step in (1, -1):
            ahead = (t - self.z) * step
            last = self.z == (0 if step == 1 else self.depth - 1)

            @pl.when((ahead > 0) & last)
            def _():
                add_rows(own, (own, self.beside[w].at[t]))
                self.send_on(w, t, step, ahead)

    def relay(self, index):
        w, t = self.sequence[index]
        own = self.own[w].at[t]
        for step in (1, -1):
            ahead = (t - self.z) * step
            behind = (self.z - step >= 0) & (self.z - step < self.depth)

            @pl.when((ahead > 0) & behind)
            def _():
                self.z_copy(w, t, step, t).wait_recv()
                add_rows(own, (own, self.beside[w].at[t], self.far[w].at[t]))
                self.send_on(w, t, step, ahead)

    def first_out(self, w):
        return sum(
            1 if self.kinds[v] == "rows" else len(self.pieces[v]) for v in range(w)
        )

    def settle(self, w):
        z, depth = self.z, self.depth
        pl.when(z > 0)(lambda: self.z_copy(w, 0, 1, z).wait_recv())
        pl.when(z < depth - 1)(lambda: self.z_copy(w, 0, 1, depth).wait_recv())
        rows = self.kinds[w] == "rows"
        target = self.outs[self.first_out(w)] if rows else self.total[self.cols.index(w)]
        home = [self.own[w].at[z], self.beside[w].at[z]]
        below, above = self.far[w].at[z], self.far[w].at[depth]
        pl.when(z == 0)(lambda: add_rows(target, (*home, above)))
        pl.when(z == depth - 1)(lambda: add_rows(target, (*home, below)))
        pl.when((z > 0) & (z < depth - 1))(lambda: add_rows(target, (*home, below, above)))
        if not rows:
            for bits in (1, 2, 3):
                self.c_copy(self.cols.index(w), bits).start()

    def spread(self, w):
        k, first = self.cols.index(w), self.first_out(w)
        for bits in (0, 1, 2, 3):
            if bits:
                self.c_copy(k, bits).wait_recv()
            source = self.total[k].at[self.c] if bits == 0 else self.block[k].at[bits - 1]
            at = 0
            for j, (size, flat) in enumerate(self.pieces[w]):
                value = source[:, at : at + size].astype(WIDE)
                if flat:
                    where = pl.ds(pl.multiple_of((self.c ^ bits) * size, 128), size)
                    self.outs[first + j][:, where] = value
                else:
                    self.outs[first + j][self.c ^ bits] = value
                at += size

    def steps(self):
        result = []
        count = len(self.sequence)
        for k in range(count + 1):
            if k < count:
                result.append((("near", k), functools.partial(self.near, k)))
            if k:
                result.append((("relay", k - 1), functools.partial(self.relay, k - 1)))
            w = k // self.depth - 1
            if k % self.depth == 0 and w >= 1:
                result.append((("settle", w - 1), functools.partial(self.settle, w - 1)))
                if w - 2 in self.cols:
                    result.append((("spread", w - 2), functools.partial(self.spread, w - 2)))
        result.append((("settle", self.n - 1), functools.partial(self.settle, self.n - 1)))
        for w in self.cols:
            if w >= self.n - 2:
                result.append((("spread", w), functools.partial(self.spread, w)))
        return result

    def finish(self):
        for w, t in self.sequence:
            self.y_copy(w, t).wait_send()
            for step in (1, -1):
                pl.when((t - self.z) * step > 0)(
                    lambda w=w, t=t, step=step: self.z_copy(w, t, step, t).wait_send()
                )
        for k in range(len(self.cols)):
            for bits in (1, 2, 3):
                self.c_copy(k, bits).wait_send()


def back_kernel(ctx_size, fsdp_size, kinds, pieces, n_out, heads, kv_heads, *refs):
    n_in = len(kinds) - 2
    parts, refs = refs[:n_in], refs[n_in:]
    far_half, out_far, w_full, w_qkv, near_half, out_near, mid, cot, refs = *refs[:8], refs[8:]
    gains, query, key, value, bias, log, rows, refs = *refs[:7], refs[7:]
    cosine, sine, normed, hidden, refs = *refs[:4], refs[4:]
    outs, refs = refs[:n_out], refs[n_out:]
    output, grad_in, gain_out, refs = *refs[:3], refs[3:]
    part_qkv, part_out, w_pad, w_proj, select, core_in, pair, pair_in, refs = *refs[:8], refs[8:]
    grad_ffn, grad_mid, mid_low, grad_rows, refs = *refs[:4], refs[4:]
    grad_key, grad_value, grad_pad, grad_low, in_near, in_far, refs = *refs[:6], refs[6:]
    last_in, swap_out, swap_in, gain_own, gain_in, gain_far, refs = *refs[:6], refs[6:]
    c_send, c_recv, g_send, g_recv, w_sem, *scratch = refs
    f, c, z, y, depth = place(fsdp_size)
    line = LineScatter(
        ctx_size, fsdp_size, kinds, pieces, (*parts, part_qkv, part_out), outs, scratch
    )
    tokens, half = query.shape[1], mid.shape[0]
    run_len, tile = half // 2, 128
    owned = part_qkv.shape[2]
    scale = HEAD_DIM**-0.5

    def exchange(index, src, dst, bits):
        return remote(src, dst, c_send.at[index], c_recv.at[index], ctx=c ^ bits)

    to_core = exchange(0, far_half, core_in, 1)
    to_x = exchange(1, pair, pair_in, 2)
    give = exchange(2, mid_low.at[pl.ds(0, half)], mid_low.at[pl.ds(half, half)], 1)
    cores = [exchange(3, in_far, last_in.at[0], 1), exchange(4, out_far, last_in.at[1], 1)]
    swaps = [exchange(5 + i, swap_out.at[i], swap_in.at[i], 2) for i in (0, 1)]
    shard = w_full.shape[1]
    piece = min(shard, HEAD_DIM)
    moves = []
    for at in range(0, heads * HEAD_DIM, piece):
        to = at // HEAD_DIM * 128 + at % HEAD_DIM
        src = w_full.at[at // shard, pl.ds(at % shard, piece)]
        moves.append(pltpu.make_async_copy(src, w_pad.at[pl.ds(to, piece)], w_sem.at[len(moves)]))
    move_proj = pltpu.make_async_copy(w_qkv, w_proj, w_sem.at[len(moves)])

    def load_weights():
        for move in moves:
            move.start()
        move_proj.start()
        for h in range(heads):
            w_pad[pl.ds(h * 128 + HEAD_DIM, 128 - HEAD_DIM)] = jnp.zeros(
                (128 - HEAD_DIM, w_pad.shape[1]), LOW
            )
        fill_select(select)

    def meet_core():
        to_core.wait_recv()
        add_rows(pair, (near_half, core_in))
        to_x.start()

    def meet_x():
        to_x.wait_recv()
        for block in (0, 1):

            def body(at, block=block):
                here = pl.ds(pl.multiple_of(at.start + block * run_len, 16), 16)
                there = pl.ds(pl.multiple_of(at.start + (1 - block) * run_len, 16), 16)
                grad = pair[here].astype(WIDE) + pair_in[there].astype(WIDE)
                grad_ffn[here] = grad
                recip = inverse_rms(mid[here])
                scaled = mid[here] * recip
                total = cot[here].astype(WIDE) + norm_backward(grad, scaled, recip, gains[1:2])
                grad_mid[here] = total
                mid_low[here] = total.astype(LOW)

            row_loop(run_len, body)
        give.start()
        for move in moves:
            move.wait()
        move_proj.wait()

    def attend_back():
        give.wait_recv()

        def back_out(at):
            grad_rows[at] = lax.dot_general(
                mid_low[at], w_pad[...], (((1,), (1,)), ((), ())), preferred_element_type=WIDE
            ).astype(LOW)

        row_loop(tokens, back_out, tile)
        grad_key[...] = jnp.zeros_like(grad_key)
        grad_value[...] = jnp.zeros_like(grad_value)

        def body(i, carry):
            h = i // (tokens // tile)
            r = i % (tokens // tile)
            at = pl.ds(pl.multiple_of(r * tile, tile), tile)
            lanes = pl.ds(pl.multiple_of(h * 128, 128), 128)
            g = h // (heads // kv_heads)
            q = query[h, at]
            s = lax.dot_general(
                q, key[g], (((1,), (1,)), ((), ())), preferred_element_type=WIDE
            )
            p = jnp.exp(s * scale + bias[at].astype(WIDE) - log[h, at])
            grad_out = grad_rows[at, lanes]
            delta = jnp.sum(
                grad_out.astype(WIDE) * rows[at, lanes].astype(WIDE), axis=-1, keepdims=True
            )
            grad_p = lax.dot_general(
                grad_out, value[g], (((1,), (1,)), ((), ())), preferred_element_type=WIDE
            )
            grad_s = (p * (grad_p - delta)).astype(LOW)
            turned = jnp.dot(grad_s, key[g], preferred_element_type=WIDE) * scale
            grad_pad[at, lanes] = turn(turned, cosine[at], -sine[at]).astype(LOW)
            grad_key[g] = grad_key[g] + contract_rows(grad_s, q)
            grad_value[g] = grad_value[g] + contract_rows(p.astype(LOW), grad_out)
            return carry

        lax.fori_loop(0, heads * (tokens // tile), body, 0)
        for g in range(kv_heads):
            for r in range(tokens // tile):
                at = pl.ds(r * tile, tile)
                turned = turn(grad_key[g, at] * scale, cosine[at], -sine[at])
                grad_pad[at, pl.ds((heads + g) * 128, 128)] = turned.astype(LOW)
                grad_pad[at, pl.ds((heads + kv_heads + g) * 128, 128)] = grad_value[g, at].astype(
                    LOW
                )

    def project_back():
        def compact(at):
            grad_low[at] = lax.dot_general(
                grad_pad[at], select[...], (((1,), (1,)), ((), ())), preferred_element_type=WIDE
            ).astype(LOW)

        row_loop(tokens, compact, tile)

        def far(at):
            there = pl.ds(pl.multiple_of(at.start + half, tile), tile)
            in_far[at] = times_transpose(grad_low[there], w_proj[...]).astype(LOW)

        row_loop(half, far, tile)
        cores[0].start()

        def near(at):
            in_near[at] = times_transpose(grad_low[at], w_proj[...])

        row_loop(half, near, tile)

    def weight_grads():
        count = w_proj.shape[0] // ctx_size
        for q in range(ctx_size):
            grads = contract_rows(normed[:, q * count : (q + 1) * count], grad_low[...]).astype(LOW)
            for e in range(fsdp_size):
                part_qkv[q, e] = grads[e * owned : (e + 1) * owned]
        for h in range(heads):
            grads = contract_rows(rows[:, h * 128 : (h + 1) * 128], mid_low[...]).astype(LOW)
            for e in range(HEAD_DIM // owned):
                part_out[h * (HEAD_DIM // owned) + e] = grads[e * owned : (e + 1) * owned]
        line.load((n_in, n_in + 1))

    near = (in_near, out_near)

    def last_core(i):
        cores[i].wait_recv()

        def body(at):
            there = pl.ds(pl.multiple_of(at.start + run_len, 16), 16)
            swap_out[i, at] = (near[i][there].astype(WIDE) + last_in[i, there].astype(WIDE)).astype(LOW)

        row_loop(run_len, body)
        swaps[i].start()

    def own_sum(i, at):
        mine = near[i][at].astype(WIDE) + last_in[i, at].astype(WIDE)
        return mine + swap_in[i, at].astype(WIDE)

    def last_in_sum():
        swaps[0].wait_recv()
        gain_own[...] = jnp.zeros_like(gain_own)

        def body(at):
            grad = own_sum(0, at)
            values = hidden[at].astype(WIDE)
            recip = inverse_rms(values)
            scaled = values * recip
            grad_in[at] = grad_mid[at] + norm_backward(grad, scaled, recip, gains[0:1])
            gain_own[0, 0:1] = gain_own[0, 0:1] + jnp.sum(grad * scaled, axis=0, keepdims=True)
            mids = mid[at]
            gain_own[0, 1:2] = gain_own[0, 1:2] + jnp.sum(
                grad_ffn[at] * (mids * inverse_rms(mids)), axis=0, keepdims=True
            )

        row_loop(run_len, body)

    def last_out_sum():
        swaps[1].wait_recv()

        def body(at):
            output[at] = (mid[at] + own_sum(1, at)).astype(LOW)

        row_loop(run_len, body)

    def gain_copy(i):
        where = ({"ctx": c ^ 1}, {"ctx": c ^ 2}, {"fsdp": f ^ 1})[i]
        return remote(gain_own.at[i], gain_in.at[i], g_send.at[i], g_recv.at[i], **where)

    def gain_row(shift):
        return remote(
            gain_own.at[3],
            gain_far.at[shift - 1],
            g_send.at[2 + shift],
            g_recv.at[2 + shift],
            fsdp=(z + shift) % depth * 2 + y,
        )

    def gain_meet(i):
        if i:
            gain_copy(i - 1).wait_recv()
            gain_own[i] = gain_own[i - 1] + gain_in[i - 1]
        if i < 3:
            gain_copy(i).start()
            return
        for shift in range(1, depth):
            gain_row(shift).start()

    def gain_end():
        total = gain_own[3]
        for shift in range(1, depth):
            gain_row(shift).wait_recv()
            total = total + gain_far[shift - 1]
        gain_out[...] = total

    greet(fsdp_size, all_rows=True)
    to_core.start()
    cores[1].start()
    line.start(n_in)
    inserts = {
        ("near", 0): [load_weights, meet_core, meet_x],
        ("near", 1): [attend_back],
        ("relay", 0): [project_back],
        ("near", 2): [lambda: last_core(0)],
        ("near", 3): [weight_grads, lambda: last_core(1)],
        ("near", 5): [last_in_sum, lambda: gain_meet(0)],
        ("near", 6): [lambda: gain_meet(1), last_out_sum],
        ("near", 7): [lambda: gain_meet(2)],
        ("near", 9): [lambda: gain_meet(3)],
    }
    weave(line.steps(), inserts)
    gain_end()
    line.finish()
    for copy in (to_core, to_x, give, *cores, *swaps, *[gain_copy(i) for i in range(3)]):
        copy.wait_send()
    for shift in range(1, depth):
        gain_row(shift).wait_send()


def turn(tensor, cosine, sine):
    lane = lax.broadcasted_iota(jnp.int32, tensor.shape, 1)
    half_dim = HEAD_DIM // 2
    moved = jnp.where(
        lane < half_dim,
        -pltpu.roll(tensor, 128 - half_dim, 1),
        pltpu.roll(tensor, half_dim, 1),
    )
    return tensor * cosine + moved * sine


def fill_select(select):
    def body(at):
        shape = (at.size, select.shape[1])
        row = lax.broadcasted_iota(jnp.int32, shape, 0) + at.start
        lane = lax.broadcasted_iota(jnp.int32, shape, 1)
        inner = lane & 127
        column = (lane >> 7) * HEAD_DIM + inner
        select[at] = jnp.where((row == column) & (inner < HEAD_DIM), 1.0, 0.0).astype(LOW)

    row_loop(select.shape[0], body, 128)


def scatter_back(ctx_size, fsdp_size, collective_id, parts, kinds, pieces, small):
    far_half, out_far, w_full, w_qkv, near_half, out_near, mid, cot = small[:8]
    gains, query, key = small[8:11]
    half, width = mid.shape
    heads, tokens, _ = query.shape
    kv_heads = key.shape[0]
    owned = width // (ctx_size * fsdp_size)
    columns = w_qkv.shape[1]
    part_qkv = jax.ShapeDtypeStruct((ctx_size, fsdp_size, owned, columns), LOW)
    part_out = jax.ShapeDtypeStruct((fsdp_size, owned, width), LOW)
    outs, chunks = LineScatter.shapes(ctx_size, (*parts, part_qkv, part_out), kinds, pieces)
    n_out = len(outs)
    run_len = half // 2
    outs += [
        jax.ShapeDtypeStruct((run_len, width), LOW),
        jax.ShapeDtypeStruct((run_len, width), WIDE),
        jax.ShapeDtypeStruct((8, width), WIDE),
    ]
    depth = fsdp_size // 2
    padded = (heads + 2 * kv_heads) * 128
    results = pl.pallas_call(
        functools.partial(back_kernel, ctx_size, fsdp_size, kinds, pieces, n_out, heads, kv_heads),
        out_shape=tuple(outs),
        in_specs=[ANY] * (len(parts) + 4) + [VMEM] * (len(small) - 4),
        out_specs=(VMEM,) * len(outs),
        scratch_shapes=[
            pltpu.VMEM(part_qkv.shape, LOW),
            pltpu.VMEM(part_out.shape, LOW),
            pltpu.VMEM((heads * 128, width), LOW),
            pltpu.VMEM(w_qkv.shape, LOW),
            pltpu.VMEM((columns, padded), LOW),
            pltpu.VMEM((half, width), LOW),
            pltpu.VMEM((half, width), LOW),
            pltpu.VMEM((half, width), LOW),
            pltpu.VMEM((half, width), WIDE),
            pltpu.VMEM((half, width), WIDE),
            pltpu.VMEM((tokens, width), LOW),
            pltpu.VMEM((tokens, heads * 128), LOW),
            pltpu.VMEM(key.shape, WIDE),
            pltpu.VMEM(key.shape, WIDE),
            pltpu.VMEM((tokens, padded), LOW),
            pltpu.VMEM((tokens, columns), LOW),
            pltpu.VMEM((half, width), WIDE),
            pltpu.VMEM((half, width), LOW),
            pltpu.VMEM((2, half, width), LOW),
            pltpu.VMEM((2, run_len, width), LOW),
            pltpu.VMEM((2, run_len, width), LOW),
            pltpu.VMEM((4, 8, width), WIDE),
            pltpu.VMEM((3, 8, width), WIDE),
            pltpu.VMEM((depth - 1, 8, width), WIDE),
            DMA((7,)),
            DMA((7,)),
            DMA((2 + depth,)),
            DMA((2 + depth,)),
            DMA((heads * HEAD_DIM // min(w_full.shape[1], HEAD_DIM) + 1,)),
            *LineScatter.scratch(fsdp_size, kinds, chunks),
        ],
        compiler_params=pltpu.CompilerParams(
            collective_id=collective_id, has_side_effects=True, vmem_limit_bytes=63 * 2**20
        ),
    )(*parts, *small)
    return results[:n_out], results[n_out:]


def inverse_rms(values):
    return lax.rsqrt(jnp.mean(values * values, axis=-1, keepdims=True) + EPS)


def norm_backward(grad_normed, scaled, inv_rms, gain):
    grad_scaled = grad_normed * gain
    return inv_rms * (
        grad_scaled - scaled * jnp.mean(grad_scaled * scaled, axis=-1, keepdims=True)
    )


def dot(left, right):
    return jnp.dot(left, right, preferred_element_type=jnp.float32)


def contract_rows(left, right):
    return lax.dot_general(
        left, right, (((0,), (0,)), ((), ())), preferred_element_type=jnp.float32
    )


def times_transpose(left, weight):
    return lax.dot_general(
        left, weight, (((1,), (1,)), ((), ())), preferred_element_type=jnp.float32
    )


def make_step(ctx_size, fsdp_size):
    def per_device(
        hidden_in,
        segments,
        w_query,
        w_key,
        w_value,
        w_out,
        w_gate,
        w_up,
        w_down,
        attn_gain,
        ffn_gain,
        grad_out,
    ):
        _, run_len, width = hidden_in.shape
        c_index, f_index = lax.axis_index("ctx"), lax.axis_index("fsdp")
        heads, kv_heads = HEADS // ctx_size, KV_HEADS // ctx_size
        q_cols, kv_cols = heads * HEAD_DIM, kv_heads * HEAD_DIM
        ff = w_gate.shape[1] // ctx_size
        shard = width // fsdp_size
        owned = shard // ctx_size
        half = 2 * run_len

        def columns(weight, size):
            return lax.dynamic_slice_in_dim(weight, c_index * size, size, 1)

        own_hidden = hidden_in.reshape(run_len, width)
        own_seg = segments.astype(WIDE)
        half_dim = HEAD_DIM // 2
        freq_index = jnp.arange(half_dim, dtype=WIDE)
        frequency = jnp.exp(freq_index * (-2.0 / HEAD_DIM) * math.log(ROPE_BASE))
        frequency = jnp.pad(jnp.concatenate([frequency, frequency]), (0, 128 - HEAD_DIM))
        (
            full_qkv,
            full_out,
            full_gate_up,
            full_down,
            _,
            cotangent,
            query,
            key,
            value,
            bias,
            cosine,
            sine,
            attn_normed,
            gains,
            attn_rows,
            log_total,
            mid,
            ffn_normed,
        ) = gather_front(
            ctx_size,
            fsdp_size,
            0,
            (
                jnp.pad(
                    jnp.stack([attn_gain, ffn_gain]).astype(WIDE), ((0, 6), (0, -shard % 128))
                ),
                jnp.concatenate(
                    [columns(w_query, q_cols), columns(w_key, kv_cols), columns(w_value, kv_cols)],
                    axis=1,
                ),
                w_out,
                jnp.concatenate([columns(w_gate, ff), columns(w_up, ff)], axis=1),
                w_down,
            ),
            (
                own_hidden,
                grad_out.reshape(run_len, width),
                jnp.broadcast_to(own_seg, (8, run_len)),
                jnp.broadcast_to(own_seg.T, (run_len, 128)),
            ),
            jnp.broadcast_to(frequency, (8, 128)),
            heads,
            kv_heads,
        )
        full_qkv = full_qkv.reshape(width, q_cols + 2 * kv_cols)
        full_gate_up = full_gate_up.reshape(width, 2 * ff)
        full_down = full_down.reshape(ff, width)
        cotangent = cotangent.reshape(-1, width)

        gate_up = dot(ffn_normed, full_gate_up)
        gate, up = gate_up[:, :ff], gate_up[:, ff:]
        sigmoid = jax.nn.sigmoid(gate)
        silu = gate * sigmoid
        inner = (silu * up).astype(LOW)
        part_output = dot(inner, full_down)
        part_down = contract_rows(inner, cotangent).astype(LOW)
        grad_inner = times_transpose(cotangent, full_down)
        grad_gate = grad_inner * up * sigmoid * (1.0 + gate * (1.0 - sigmoid))
        grad_gate_up = jnp.concatenate(
            [grad_gate.astype(LOW), (grad_inner * silu).astype(LOW)], axis=1
        )
        part_ffn = times_transpose(grad_gate_up, full_gate_up)
        part_gate_up = contract_rows(ffn_normed, grad_gate_up).astype(LOW)

        grads, (output, grad_in, gain_sums) = scatter_back(
            ctx_size,
            fsdp_size,
            1,
            (
                part_gate_up.reshape(ctx_size, fsdp_size, owned, 2 * ff),
                part_down.reshape(fsdp_size, -1, width),
            ),
            ("cols", "rows", "cols", "rows"),
            (((ff, True), (ff, True)), None, ((q_cols, True), (2 * kv_cols, False)), None),
            (
                part_ffn[half:].astype(LOW),
                part_output[half:].astype(LOW),
                full_out,
                full_qkv,
                part_ffn[:half],
                part_output[:half].astype(LOW),
                mid,
                cotangent[:half],
                gains,
                query,
                key,
                value,
                bias,
                log_total,
                attn_rows,
                cosine,
                sine,
                attn_normed,
                own_hidden,
            ),
        )
        grad_gate_w, grad_up_w, grad_down_w, grad_query_w, grad_kv_w, grad_out_w = grads
        grad_kv_w = jnp.swapaxes(grad_kv_w, 0, 1)
        gain_own = lax.dynamic_slice_in_dim(
            gain_sums[:2], (c_index * fsdp_size + f_index) * owned, owned, 1
        )

        return (
            output[None],
            grad_in[None],
            grad_query_w,
            grad_kv_w[:, :, :kv_cols].reshape(owned, -1),
            grad_kv_w[:, :, kv_cols:].reshape(owned, -1),
            grad_out_w,
            grad_gate_w,
            grad_up_w,
            grad_down_w,
            gain_own[0],
            gain_own[1],
        )

    return per_device


def solution(mesh):
    rows = P("fsdp", None)
    spread = P(("ctx", "fsdp"), None)
    runs = P("fsdp", "ctx", None)
    return jax.shard_map(
        make_step(mesh.shape["ctx"], mesh.shape["fsdp"]),
        mesh=mesh,
        in_specs=(runs, P("fsdp", "ctx"), *[rows] * 7, P("fsdp"), P("fsdp"), runs),
        out_specs=(runs, runs, *[spread] * 7, P(("ctx", "fsdp")), P(("ctx", "fsdp"))),
        check_vma=False,
    )
```

time: 477 us -> 373 us (0.78)
  Pallas kernels: 382 us -> 327 us
  local copies, waits for them, and re-layouts: 42.6 us -> 18.9 us
  other arithmetic: 14.5 us -> 2.46 us
  matrix products: 31.6 us -> 23.3 us
    pallas_call x4 -> x2, Pallas kernels: 382 us -> 327 us  [the longest x1 186 us: scatter_back(): pl.pallas_call(functools.partial(back_kernel, ctx_size, fsdp_size, kinds,...]
    slice x16 -> x1, local copies, waits for them, and re-layouts: 15 us -> 1.24 us  [per_device(): part_output[:half].astype(LOW)]
    unnamed x67 -> x41, local copies, waits for them, and re-layouts: 14.7 us -> 5.78 us
    dot_general x4 -> x2, matrix products: 13 us -> 9.11 us  [contract_rows(): lax.dot_general(left, right, (((0,), (0,)), ((), ())), preferred_element_...]
where the time goes in v1:
time: 373 us
  Pallas kernels  327 us (88%)
  matrix products  23.3 us (6%)
  local copies, waits for them, and re-layouts  18.9 us (5%)
    pallas_call x1, Pallas kernels, scatter_back(): pl.pallas_call(functools.partial(back_kernel, ctx_size, fsdp_size, kinds,...  186 us
    pallas_call x1, Pallas kernels, gather_front(): pl.pallas_call(functools.partial(front_kernel, ctx_size, fsdp_size, tuple...  141 us
    dot_general x2, matrix products, contract_rows(): lax.dot_general(left, right, (((0,), (0,)), ((), ())), preferred_element_...  9.11 us
    dot_general x2, matrix products, dot(): return jnp.dot(left, right, preferred_element_type=jnp.float32)  8.11 us

profile of v1, /device:TPU:0, one launch (start us, length us, event | category | flops | bytes accessed | tf_op | source)
XLA Modules:
  0.0 372.8 jit_solution(14887212658054694343)
XLA Ops:
  0.6 0.0 copy-start
  0.7 1.2 constant_dynamic-slice_fusion.3
  1.8 0.0 copy-start.12
  1.9 0.0 copy-start.13
  1.9 0.0 copy-start.14
  1.9 0.0 copy-done
  1.9 0.8 pad_maximum_fusion.4.refs_1_
  2.7 1.2 constant_dynamic-slice_fusion.1
  3.9 0.9 pad_maximum_fusion.3.refs_3_
  4.9 0.7 broadcast_in_dim.23.refs_8_
  5.6 0.6 broadcast_in_dim.22.refs_7_
  6.2 0.0 copy-done.14
  6.2 0.6 fusion.8.refs_0_
  6.8 0.1 fusion.9
  6.9 0.6 broadcast_in_dim.24.refs_9_
  7.5 141.4 %shard_map.203 = (bf16[8,192,768]{2,1,0:T(8,128)(2,1)}, bf16[2,192,1536]{2,1,0:T(8,128)(2,1)}, bf16[8,192,2048]{2,1,0:T(8,128)(2,1)}, bf16[2,512,1536]{2,1,0:T(8...) custom-call(f32[8,256]{1,0:T(8,128)} %fusion.8.refs_0_, ...), custom_call_target="tpu_custom_call" | custom-call | tf_op jit(solution)/shard_map/pallas_call | solution.py:522
  148.9 0.0 copy-start.6
  148.9 0.0 copy-start.10
  148.9 0.0 slice-start
  148.9 6.3 %fusion.14 = f32[512,2048]{1,0:T(8,128)S(1)} fusion(bf16[512,1536]{1,0:T(8,128)(2,1)} %get-tuple-element.37, bf16[1536,2048]{1,0:T(8,128)(2,1)} %bitcast.40), kind=kOutput, calls=%fused_computation.39 | convolution fusion | flops 3221225472 | bytes 12058624 | tf_op jit(solution)/shard_map/dot_general | solution.py:1100
  155.3 0.0 slice-start.1
  155.3 2.6 multiply_convert_fusion.2
  157.9 1.8 convolution_convert_fusion.2
  159.7 1.2 fusion.12
  160.9 3.5 fusion.1
  164.4 1.3 slice.59.refs_6_
  165.7 1.0 slice.74.refs_2_
  166.6 3.6 convolution_convert_fusion.1
  170.2 0.0 copy-done.11
  170.2 5.5 %convolution_convert_fusion = bf16[1536,2048]{1,0:T(8,128)(2,1)} fusion(bf16[512,1536]{1,0:T(8,128)(2,1)S(1)} %copy-done.11, bf16[512,1024]{1,0:T(8,128)(2,1)S(1)} %get-tuple-element.64, bf16[512,1024]{1,0:T(8,128)(2,1)S(1)} %get-tuple-element.63), kind=kOutput, calls=%fused_computation | convolution fusion | flops 3228565504 | bytes 9961472 | tf_op jit(solution)/shard_map/dot_general | solution.py:1104
  175.7 0.9 slice.48
  176.7 185.8 %shard_map.204 = (f32[48,4096]{1,0:T(8,128)}, f32[48,4096]{1,0:T(8,128)}, f32[128,1536]{1,0:T(8,128)}, f32[48,1536]{1,0:T(8,128)}, f32[4,48,384]{2,1,0:T(8,128)}...) custom-call(bf16[4,8,48,2048]{3,2,1,0:T(8,128)(2,1)} %bitcast.28, ...), custom_call_target="tpu_custom_call" | custom-call | tf_op jit(solution)/shard_map/pallas_call | solution.py:1044
  362.5 1.2 fusion.13
  363.8 0.1 copy.23
  363.9 0.8 reshape.62
  364.7 0.1 copy.24
  364.9 0.8 reshape.63
  365.7 0.8 slice.52
  366.5 0.1 constant_dynamic-slice_fusion
  366.5 0.5 slice_bitcast_fusion
  367.1 0.0 copy-done.7
  367.1 0.7 copy.32
  367.8 0.9 copy.33
  368.7 0.7 copy.34
  369.4 0.7 copy.35
  370.1 0.9 copy.36
  371.0 0.9 copy.37
  371.9 0.9 copy.38
  (28 shorter events, 0.1 us)
Async XLA Ops:
  0.6 1.2 copy-start
  1.8 3.0 copy-start.12
  1.9 4.3 %copy-start.13 = (bf16[192]{0:T(256)(128)(2,1)S(1)}, bf16[192]{0:T(256)(128)(2,1)}, u32[]{:S(2)}) copy-start(bf16[192]{0:T(256)(128)(2,1)} %param.22) | copy-start | bytes 1156
  1.9 4.3 %copy-start.14 = (bf16[192]{0:T(256)(128)(2,1)S(1)}, bf16[192]{0:T(256)(128)(2,1)}, u32[]{:S(2)}) copy-start(bf16[192]{0:T(256)(128)(2,1)} %param.21) | copy-start | bytes 1156
  148.9 6.4 %copy-start.6 = (bf16[4,128,1536]{2,1,0:T(8,128)(2,1)S(1)}, bf16[4,128,1536]{2,1,0:T(8,128)(2,1)}, u32[]{:S(2)}) copy-start(bf16[4,128,1536]{2,1,0:T(8,128)(2,1)} %get-tuple-element.38) | copy-start | bytes 4718596
  148.9 6.4 %copy-start.10 = (bf16[2,512,1536]{2,1,0:T(8,128)(2,1)S(1)}, bf16[2,512,1536]{2,1,0:T(8,128)(2,1)}, u32[]{:S(2)}) copy-start(bf16[2,512,1536]{2,1,0:T(8,128)(2,1)} %get-tuple-element.39) | copy-start | bytes 9437188
  148.9 12.0 %slice-start = ((s8[6291456]{0:T(1024)(128)(4,1)}), s8[4194304]{0:T(1024)(128)(4,1)S(1)}, s32[]{:S(2)}) async-start(s8[6291456]{0:T(1024)(128)(4,1)} %bitcast.41), calls=%async_computation | async-start | bytes 8388608
  155.3 5.6 %slice-start.1 = ((s8[6291456]{0:T(1024)(128)(4,1)}), s8[2097152]{0:T(1024)(128)(4,1)S(1)}, s32[]{:S(2)}) async-start(s8[6291456]{0:T(1024)(128)(4,1)} %bitcast.41), calls=%async_computation.1 | async-start | bytes 4194304
  166.6 3.6 copy-start.11
  362.5 4.5 %copy-start.7 = (bf16[128,1536]{1,0:T(8,128)(2,1)S(1)}, bf16[128,1536]{1,0:T(8,128)(2,1)}, u32[]{:S(2)}) copy-start(bf16[128,1536]{1,0:T(8,128)(2,1)} %get-tuple-element.54) | copy-start | bytes 1179652
  362.5 5.3 %copy-start.5 = (f32[128,1536]{1,0:T(8,128)S(1)}, f32[128,1536]{1,0:T(8,128)}, u32[]{:S(2)}) copy-start(f32[128,1536]{1,0:T(8,128)} %get-tuple-element.55) | copy-start | bytes 2359300
  363.8 4.9 %copy-start.9 = (f32[48,1536]{1,0:T(8,128)S(1)}, f32[48,1536]{1,0:T(8,128)}, u32[]{:S(2)}) copy-start(f32[48,1536]{1,0:T(8,128)} %get-tuple-element.89) | copy-start | bytes 884740
  363.9 5.5 %copy-start.8 = (f32[48,1536]{1,0:T(8,128)S(1)}, f32[48,1536]{1,0:T(8,128)}, u32[]{:S(2)}) copy-start(f32[48,1536]{1,0:T(8,128)} %get-tuple-element.92) | copy-start | bytes 884740
  364.7 5.4 %copy-start.4 = (f32[48,4096]{1,0:T(8,128)S(1)}, f32[48,4096]{1,0:T(8,128)}, u32[]{:S(2)}) copy-start(f32[48,4096]{1,0:T(8,128)} %get-tuple-element.93) | copy-start | bytes 2359300
  367.8 3.2 copy-start.3
  368.7 3.2 copy-start.2
  369.4 3.4 copy-start.1
